TPU v7x, 32 devices: a whole 2x2x4 slice. The times are simulated.
32 devices in a mesh: swath: 8 (over y, x, core), chan: 4 (over z).
Axes of the slice: x: 2, y: 2, z: 4, core: 2. Of those that a mesh axis runs over, the one named last changes fastest.
Arguments:
- innovations: float32 [524288], P(('swath', 'chan')), may hold values from -6 to 6
- obs_precision: float32 [524288], P(('swath', 'chan')), may hold values from 0.25 to 4
- jacobian: bfloat16 [524288, 128], P(('swath', 'chan')), may hold values from -0.5 to 0.5
- predictors: float32 [8, 524288], P(None, ('swath', 'chan')), may hold values from -5 to 5
- obs_column: int32 [524288], P(('swath', 'chan')), may hold values from 0 to 2047, as said below
- obs_channel: int32 [524288], P(('swath', 'chan')), may hold values from 0 to 5119
- obs_count: int32 [8, 4], P('swath', 'chan'), may hold values from 5461 to 16384, as said below
- smoothing: float32 [128], replicated, may hold values from 0.02 to 0.12
- bias_precision: float32 [8, 5120], P(None, 'chan'), may hold values from 1 to 100
Outputs:
- control_state: float32 [256, 256, 128], P('swath', 'chan')
- bias_increment: float32 [8, 5120], P(None, 'chan')
- residual_norms: float32 [3], replicated
Inputs may be any that keep to these rules, and one draw needn't show every extreme that they name: `obs_column`: Row-major index latitude row * 64 + longitude column within the tile of the device that holds the slot; all slots of an aligned block of 128 slots lie in one latitude row. `obs_channel`: channel c belongs to block c // 256, whose coefficients are owned by chan index c // 1280. `obs_count`: slots below the count hold live observations, the rest are ignored; some device is full in every draw.
All inputs are finite; a program needn't handle non-finite values.
Results may differ from a plain program's by a relative error of at most 0.0003.
Values sent between devices are 32-bit elements; how exact they have to be, the bound alone decides.
No kernel may reach another device: no remote copies, remote signals or barrier semaphores. Data moves between devices by JAX's collectives and lax.ppermute only.
A program may use at most 128 MiB of HBM per device.

v0:
```python
import jax
import jax.numpy as jnp
from jax import lax
from jax.sharding import PartitionSpec as P

LEV = 128
NPRED = 8
CH_BLOCK = 256
OBS_BLOCK = 128
LAT_DEV = 32
LON_DEV = 64
ITERS = 2


def with_halo(array, sides, width):
    for axis, dim in sides:
        size, length = (lax.axis_size(axis), array.shape[dim])
        up = [(i, (i + 1) % size) for i in range(size)]
        down = [(j, i) for i, j in up]
        last = lax.slice_in_dim(array, length - width, length, axis=dim)
        leading = lax.slice_in_dim(array, 0, width, axis=dim)
        before = lax.ppermute(last, axis, up)
        after = lax.ppermute(leading, axis, down)
        array = jnp.concatenate([before, array, after], axis=dim)
    return array


def body(
    innovations,
    obs_precision,
    jacobian,
    predictors,
    obs_column,
    obs_channel,
    obs_count,
    smoothing,
    bias_precision,
):
    owned_width = bias_precision.shape[1]
    channels_all = owned_width * lax.axis_size("chan")
    block_ids = channels_all // CH_BLOCK
    slot_total = obs_precision.shape[0]
    line_count = slot_total // OBS_BLOCK
    band_index = lax.axis_index("swath")
    top_keep = band_index > 0
    bottom_keep = band_index < lax.axis_size("swath") - 1
    bias_weight = jnp.where(band_index == 0, 1.0, 0.0).astype(jnp.float32)
    live = jnp.arange(slot_total, dtype=jnp.int32) < obs_count[0, 0]
    weights = jnp.where(live, obs_precision, 0.0)
    row_ids = jnp.arange(LAT_DEV)
    keep_above = ((row_ids > 0) | top_keep)[:, None, None]
    keep_below = ((row_ids < LAT_DEV - 1) | bottom_keep)[:, None, None]
    highest = lax.Precision.HIGHEST
    line_cells = obs_column.reshape(line_count, OBS_BLOCK)
    line_row = line_cells[:, 0] // LON_DEV
    row_hot = (line_row[:, None] == jnp.arange(LAT_DEV, dtype=jnp.int32)[None, :]).astype(
        jnp.float32
    )
    col_hot = (
        (line_cells % LON_DEV)[:, :, None] == jnp.arange(LON_DEV, dtype=jnp.int32)[None, None, :]
    ).astype(jnp.float32)
    jac_lines = jacobian.reshape(line_count, OBS_BLOCK, LEV).astype(jnp.float32)
    block_hot = (
        (obs_channel // CH_BLOCK)[:, None] == jnp.arange(block_ids, dtype=jnp.int32)[None, :]
    ).astype(jnp.float32)
    inner_hot = (
        (obs_channel % CH_BLOCK)[:, None] == jnp.arange(CH_BLOCK, dtype=jnp.int32)[None, :]
    ).astype(jnp.float32)

    def smooth_local(state_field):
        padded = with_halo(state_field, (("swath", 0), ("chan", 1)), 1)
        above_row = jnp.where(keep_above, padded[:-2, 1:-1], 0.0)
        below_row = jnp.where(keep_below, padded[2:, 1:-1], 0.0)
        beside = above_row + below_row + padded[1:-1, :-2] + padded[1:-1, 2:]
        return state_field + smoothing * (beside - 4.0 * state_field)

    def adjoint(values):
        terms = jac_lines * values.reshape(line_count, OBS_BLOCK)[:, :, None]
        line_fields = jnp.einsum("box,bok->bxk", col_hot, terms, precision=highest)
        return jnp.einsum("bl,bxk->lxk", row_hot, line_fields, precision=highest)

    def partial_table(terms):
        rows_in = terms.shape[0]
        spread = (terms[:, None, :] * block_hot.T[None, :, :]).reshape(
            rows_in * block_ids, slot_total
        )
        table = jnp.dot(spread, inner_hot, precision=highest)
        return table.reshape(rows_in, channels_all)

    def to_owners(partial_value):
        owned = lax.psum_scatter(partial_value, "chan", scatter_dimension=1, tiled=True)
        return lax.psum(owned, "swath")

    def inner(state_one, state_two, bias_one, bias_two):
        return jnp.sum(state_one * state_two) + bias_weight * jnp.sum(bias_one * bias_two)

    source = weights * innovations
    stacked = to_owners(
        partial_table(
            jnp.concatenate(
                [predictors * source[None, :], predictors * predictors * weights[None, :]], axis=0
            )
        )
    )
    res_state = smooth_local(adjoint(source))
    res_bias = stacked[:NPRED]
    diagonal = bias_precision + stacked[NPRED:]
    sol_state = jnp.zeros_like(res_state)
    sol_bias = jnp.zeros_like(res_bias)
    pre_bias = res_bias / diagonal
    record = []

    def norms_of(state_res, bias_res, bias_pre):
        return lax.psum(
            (
                inner(state_res, state_res, bias_res, bias_pre),
                inner(state_res, state_res, bias_res, bias_res),
            ),
            ("swath", "chan"),
        )

    rz_now, rr_now = norms_of(res_state, res_bias, pre_bias)
    record.append(rr_now)
    dir_state, dir_bias = (res_state, pre_bias)
    for turn_index in range(ITERS):
        smoothed = smooth_local(dir_state)
        hessian_everything = lax.all_gather(dir_bias, "chan", axis=1, tiled=True)
        flat = hessian_everything.reshape(NPRED * block_ids, CH_BLOCK)
        mid = jnp.dot(inner_hot, flat.T, precision=highest).reshape(slot_total, NPRED, block_ids)
        looked = jnp.sum(mid * predictors.T[:, :, None] * block_hot[:, None, :], axis=(1, 2))
        forward_line_fields = jnp.einsum("bl,lxk->bxk", row_hot, smoothed, precision=highest)
        picked = jnp.einsum("box,bxk->bok", col_hot, forward_line_fields, precision=highest)
        image = weights * (jnp.sum(jac_lines * picked, axis=2).reshape(-1) + looked)
        state_out = dir_state + smooth_local(adjoint(image))
        bias_out = bias_precision * dir_bias + to_owners(partial_table(predictors * image[None, :]))
        curve = lax.psum(inner(dir_state, state_out, dir_bias, bias_out), ("swath", "chan"))
        length = rz_now / curve
        sol_state = sol_state + length * dir_state
        sol_bias = sol_bias + length * dir_bias
        res_state = res_state - length * state_out
        res_bias = res_bias - length * bias_out
        pre_bias = res_bias / diagonal
        rz_next, rr_now = norms_of(res_state, res_bias, pre_bias)
        record.append(rr_now)
        ratio = rz_next / rz_now
        dir_state = res_state + ratio * dir_state
        dir_bias = pre_bias + ratio * dir_bias
        rz_now = rz_next
    return (sol_state, sol_bias, jnp.sqrt(jnp.stack(record)))


def solution(mesh):
    placed = (
        P(("swath", "chan")),
        P(("swath", "chan")),
        P(("swath", "chan"), None),
        P(None, ("swath", "chan")),
        P(("swath", "chan")),
        P(("swath", "chan")),
        P("swath", "chan"),
        P(),
        P(None, "chan"),
    )
    return jax.shard_map(
        body,
        mesh=mesh,
        in_specs=placed,
        out_specs=(P("swath", "chan", None), P(None, "chan"), P()),
        check_vma=False,
    )
```

profile of v0, /device:TPU:0, one launch (start us, length us, event | category | flops | bytes accessed | tf_op | source)
XLA Modules:
  0.0 604.4 jit_solution(15087410023057047075)
XLA Ops:
  10.6 7.1 %fusion.17 = f32[128,64,128]{2,1,0:T(8,128)S(1)} fusion(bf16[128,128,128]{2,1,0:T(8,128)(2,1)} %bitcast.41, f32[128,128]{1,0:T(8,128)S(1)} %bitcast.49, s32[128,128]{1,0:T(8,128)S(1)} %add_select_fusion.2), kind=kOutput, calls=%fused_computation.21 | convolution fusion | flops 1615855616 | bytes 8519680 | tf_op jit(solution)/shard_map/box,bok->bxk/dot_general | solution.py:79
  17.7 3.9 fusion.30
  22.3 3.4 collective-permute-start.1
  26.0 8.5 %broadcast_multiply_fusion = f32[16,20,16384]{2,1,0:T(8,128)} fusion(f32[20,16384]{1,0:T(8,128)S(1)} %fusion.50, f32[16,16384]{1,0:T(8,128)S(1)} %pad_maximum_fusion.48), kind=kLoop, calls=%fused_computation.9 | loop fusion | flops 5242880 | bytes 23330816 | tf_op jit(solution)/shard_map/mul | solution.py:84
  35.2 3.6 collective-permute-start.3
  38.8 17.1 %mul.337 = f32[320,16384]{1,0:T(8,128)} reshape(f32[16,20,16384]{2,1,0:T(8,128)} %broadcast_multiply_fusion) | data formatting | bytes 41943040 | tf_op jit(solution)/shard_map/mul | solution.py:84
  58.1 2.4 collective-permute-start.5
  60.5 16.8 %fusion.5 = f32[320,256]{1,0:T(8,128)} fusion(f32[320,16384]{1,0:T(8,128)} %mul.337, s32[16384]{0:T(1024)S(1)} %get-tuple-element.55), kind=kOutput, calls=%fused_computation.8 | convolution fusion | flops 16110321664 | bytes 21364736 | tf_op jit(solution)/shard_map/dot_general | solution.py:87
  77.3 1.8 reshape.130
  79.9 3.6 collective-permute-start.7
  85.3 7.0 %copy.21 = f32[128,128,128]{1,2,0:T(8,128)} copy(bf16[128,128,128]{2,1,0:T(8,128)(2,1)} %bitcast.42) | data formatting | bytes 12582912 | tf_op jit(solution)/shard_map/convert_element_type | solution.py:62
  92.3 7.2 %fusion.91 = f32[128,64,128]{2,0,1:T(8,128)} fusion(f32[32,64,128]{2,0,1:T(8,128)} %copy-done.9, f32[34,1,128]{2,0,1:T(8,128)} %collective-permute-done.7, f32[1,64,128]{2,0,1:T(1,128)S(1)} %collective-permute-done.5, f32[1,64,128]{2,0,1:T(1,128)} %collective-permute-done.4, f32[34,1,128]{2,0,1:T(8,128)} %collective-permute-done.6, f32[128]{0:T(128)S(1)} %copy-done.31, ...), kind=kOutput, calls=%fused_computation.113 | convolution fusion | flops 407113728 | bytes 5344320 | tf_op jit(solution)/shard_map/bl,lxk->bxk/dot_general | solution.py:131
  101.3 11.4 %multiply_reduce_fusion.1 = f32[128,128]{1,0:T(8,128)S(1)} fusion(f32[128,128,128]{1,2,0:T(8,128)} %copy.21, f32[128,64,128]{2,0,1:T(8,128)} %fusion.91, s32[128,128]{1,0:T(8,128)S(1)} %add_select_fusion.2), kind=kOutput, calls=%fused_computation.15 | convolution fusion | flops 1615839232 | bytes 12713984 | tf_op jit(solution)/shard_map/box,bxk->bok/dot_general | solution.py:132
  112.7 40.4 %all-reduce.4.cloned.1.call-done = f32[16,1280]{1,0:T(8,128)} async-done(((f32[16,1280]{1,0:T(8,128)}), f32[16,1280]{1,0:T(8,128)}) %all-reduce.4.cloned.1.call-update) | async-done | bytes 81936 | tf_op jit(solution)/shard_map/psum | solution.py:92
  153.9 14.0 %all_gather.6 = f32[8,5120]{1,0:T(8,128)S(1)} all-gather(f32[8,1280]{1,0:T(8,128)S(1)} %slice_divide_fusion), channel_id=1, replica_groups=mesh['swath'=8,'chan'=4] {'chan'}, dimensions={1}, use_global_device_ids=true | all-gather | bytes 204800 | tf_op jit(solution)/shard_map/all_gather | solution.py:127
  167.9 12.2 %fusion.35 = f32[16384]{0:T(1024)S(1)} fusion(f32[16384,20]{0,1:T(8,128)} %fusion.51, f32[16384,8]{0,1:T(8,128)S(1)} %bitcast.45, s32[16384]{0:T(1024)S(1)} %get-tuple-element.55, f32[8,20,256]{2,0,1:T(8,128)S(1)} %bitcast.52), kind=kOutput, calls=%fused_computation.42 | convolution fusion | flops 8065105920 | bytes 2129920 | tf_op jit(solution)/shard_map/dot_general | solution.py:129
  180.3 5.9 fusion.10
  186.1 3.9 fusion.26
  192.2 5.9 broadcast_multiply_fusion.2
  198.1 8.7 %mul.360 = f32[160,16384]{1,0:T(8,128)} reshape(f32[8,20,16384]{2,1,0:T(8,128)} %broadcast_multiply_fusion.2) | data formatting | bytes 20971520 | tf_op jit(solution)/shard_map/mul | solution.py:84
  208.3 3.4 collective-permute-start.11
  212.0 11.9 %fusion.3 = f32[160,256]{1,0:T(8,128)} fusion(f32[160,16384]{1,0:T(8,128)} %mul.360, s32[16384]{0:T(1024)S(1)} %get-tuple-element.55), kind=kOutput, calls=%fused_computation.6 | convolution fusion | flops 8057257984 | bytes 10715136 | tf_op jit(solution)/shard_map/dot_general | solution.py:87
  225.8 6.8 %multiply_reduce_fusion.5 = (f32[]{:T(128)}, f32[]{:T(128)}, f32[32,64,128]{2,0,1:T(8,128)}) fusion(f32[32,64,128]{2,0,1:T(8,128)} %copy-done.5, f32[34,1,128]{2,0,1:T(8,128)} %collective-permute-done.11, f32[1,64,128]{2,0,1:T(1,128)} %copy-done.18, f32[1,64,128]{2,0,1:T(1,128)} %copy-done.19, f32[34,1,128]{2,0,1:T(8,128)} %collective-permute-done.10, ...), kind=kLoop, calls=%fused_computation.153 | loop fusion | flops 10223614 | bytes 3347016 | tf_op jit(solution)/shard_map/reduce_sum | solution.py:95
  232.6 13.9 %reduce-scatter.6.cloned.1.call-done = f32[8,1280]{1,0:T(8,128)} async-done(((f32[8,5120]{1,0:T(8,128)}), f32[8,1280]{1,0:T(8,128)}) %reduce-scatter.6.cloned.1.call-update) | async-done | bytes 40976 | tf_op jit(solution)/shard_map/reduce_scatter | solution.py:91
  246.5 23.9 %psum.72 = f32[8,1280]{1,0:T(8,128)} all-reduce(f32[8,1280]{1,0:T(8,128)} %reduce-scatter.6.cloned.1.call-done), channel_id=1, replica_groups=mesh['swath'=8,'chan'=4] {'swath'}, use_global_device_ids=true, to_apply=%region_9.10 | all-reduce | flops 10240 | bytes 81920 | tf_op jit(solution)/shard_map/psum | solution.py:92
  274.5 37.6 %all-reduce.1 = (f32[]{:T(128)}, f32[]{:T(128)}) all-reduce(f32[]{:T(128)S(6)} %add.166, f32[]{:T(128)S(6)} %add.178), channel_id=1, replica_groups=mesh['swath'=8,'chan'=4] {'swath','chan'}, use_global_device_ids=true, to_apply=%region_4.5 | all-reduce | flops 2 | bytes 16 | tf_op jit(solution)/shard_map/psum | solution.py:114
  313.4 2.1 multiply_reduce_fusion.11
  316.1 2.6 multiply_reduce_fusion.4
  319.4 42.3 %psum.74 = f32[]{:T(128)} all-reduce(f32[]{:T(128)S(6)} %add.179), channel_id=1, replica_groups=mesh['swath'=8,'chan'=4] {'swath','chan'}, use_global_device_ids=true, to_apply=%region_14.15 | all-reduce | flops 1 | bytes 8 | tf_op jit(solution)/shard_map/psum | solution.py:114
  363.0 2.0 multiply_add_fusion.1
  367.1 13.7 %all_gather.7 = f32[8,5120]{1,0:T(8,128)S(1)} all-gather(f32[8,1280]{1,0:T(8,128)S(1)} %multiply_add_fusion.4), channel_id=1, replica_groups=mesh['swath'=8,'chan'=4] {'chan'}, dimensions={1}, use_global_device_ids=true | all-gather | bytes 204800 | tf_op jit(solution)/shard_map/all_gather | solution.py:127
  384.1 11.7 %fusion.38 = f32[16384]{0:T(1024)} fusion(f32[16384,20]{0,1:T(8,128)S(1)} %copy-done.10, f32[16384,8]{0,1:T(8,128)S(1)} %bitcast.46, s32[16384]{0:T(1024)S(1)} %get-tuple-element.55, f32[8,20,256]{2,0,1:T(8,128)S(1)} %bitcast.51), kind=kOutput, calls=%fused_computation.43 | convolution fusion | flops 8065105920 | bytes 2129920 | tf_op jit(solution)/shard_map/dot_general | solution.py:129
  396.5 5.3 fusion.65
  401.8 11.9 %multiply_reduce_fusion = f32[128,128]{1,0:T(8,128)S(1)} fusion(f32[128,128,128]{1,2,0:T(8,128)} %copy.21, f32[128,64,128]{2,0,1:T(8,128)S(1)} %fusion.65, s32[128,128]{1,0:T(8,128)S(1)} %add_select_fusion.2), kind=kOutput, calls=%fused_computation.12 | convolution fusion | flops 1615839232 | bytes 12713984 | tf_op jit(solution)/shard_map/box,bxk->bok/dot_general | solution.py:132
  413.8 5.9 fusion.8
  419.7 3.9 fusion.22
  425.2 5.9 broadcast_multiply_fusion.1
  431.1 8.8 %mul.392 = f32[160,16384]{1,0:T(8,128)} reshape(f32[8,20,16384]{2,1,0:T(8,128)} %broadcast_multiply_fusion.1) | data formatting | bytes 20971520 | tf_op jit(solution)/shard_map/mul | solution.py:84
  440.6 3.4 collective-permute-start.19
  444.3 12.0 %fusion.2 = f32[160,256]{1,0:T(8,128)} fusion(f32[160,16384]{1,0:T(8,128)} %mul.392, s32[16384]{0:T(1024)S(1)} %get-tuple-element.55), kind=kOutput, calls=%fused_computation.5 | convolution fusion | flops 8057257984 | bytes 10715136 | tf_op jit(solution)/shard_map/dot_general | solution.py:87
  456.3 1.7 reshape.134
  458.1 5.6 multiply_reduce_fusion.3
  463.7 15.0 %reduce-scatter.8.cloned.1.call-done = f32[8,1280]{1,0:T(8,128)} async-done(((f32[8,5120]{1,0:T(8,128)}), f32[8,1280]{1,0:T(8,128)}) %reduce-scatter.8.cloned.1.call-update) | async-done | bytes 40976 | tf_op jit(solution)/shard_map/reduce_scatter | solution.py:91
  478.7 23.3 %psum.75 = f32[8,1280]{1,0:T(8,128)S(1)} all-reduce(f32[8,1280]{1,0:T(8,128)} %reduce-scatter.8.cloned.1.call-done), channel_id=1, replica_groups=mesh['swath'=8,'chan'=4] {'swath'}, use_global_device_ids=true, to_apply=%region_19.20 | all-reduce | flops 10240 | bytes 81920 | tf_op jit(solution)/shard_map/psum | solution.py:92
  504.4 37.5 %psum.76 = f32[]{:T(128)} all-reduce(f32[]{:T(128)S(6)} %add.193), channel_id=1, replica_groups=mesh['swath'=8,'chan'=4] {'swath','chan'}, use_global_device_ids=true, to_apply=%region_21.22 | all-reduce | flops 1 | bytes 8 | tf_op jit(solution)/shard_map/psum | solution.py:136
  544.6 2.7 multiply_reduce_fusion.2
  551.5 43.7 %all-reduce = (f32[1]{0:T(128)}, f32[1]{0:T(128)}, f32[1]{0:T(128)}) all-reduce(f32[1]{0:T(128)} %bitcast.16, f32[1]{0:T(128)} %bitcast.15, f32[1]{0:T(128)} %bitcast.14), channel_id=1, replica_groups=mesh['swath'=8,'chan'=4] {'swath','chan'}, use_global_device_ids=true, to_apply=%region_28.29 | all-reduce | flops 3 | bytes 24 | tf_op jit(solution)/shard_map/psum | solution.py:114
  595.2 2.5 maximum_sqrt_fusion
  (150 shorter events, 30.3 us)
Async XLA Ops:
  7.2 94.0 %reduce-scatter.4.cloned.1.call-start = ((), (), s32[]{:S(2)}) async-start(), calls=%async_computation.3 | async-start | bytes 409600 | tf_op jit(solution)/shard_map/reduce_scatter | solution.py:91
  17.7 8.1 %copy-start.8 = (f32[8,16384]{1,0:T(8,128)S(1)}, f32[8,16384]{1,0:T(8,128)}, u32[]{:S(2)}) copy-start(f32[8,16384]{1,0:T(8,128)} %param.12) | copy-start | bytes 1572868
  22.3 12.2 %collective-permute-start.1 = (f32[1,64,128]{2,0,1:T(1,128)}, f32[1,64,128]{2,0,1:T(1,128)S(1)}, u32[]{:S(2)}, u32[]{:S(2)}) collective-permute-start(f32[1,64,128]{2,0,1:T(1,128)} %get-tuple-element.52), channel_id=1, source_target_pairs={{4,0},{8,4},{12,8},{16,12},{20,16},{24,20},{28,24},{0,28},{5,1},{9... | collective-permute-start | bytes 98312 | tf_op jit(solution)/shard_map/ppermute | solution.py:23
  25.7 8.9 %collective-permute-start = (f32[1,64,128]{2,0,1:T(1,128)}, f32[1,64,128]{2,0,1:T(1,128)S(1)}, u32[]{:S(2)}, u32[]{:S(2)}) collective-permute-start(f32[1,64,128]{2,0,1:T(1,128)} %get-tuple-element.51), channel_id=1, source_target_pairs={{0,4},{4,8},{8,12},{12,16},{16,20},{20,24},{24,28},{28,0},{1,5},{5... | collective-permute-start | bytes 98312 | tf_op jit(solution)/shard_map/ppermute | solution.py:22
  35.2 20.7 %collective-permute-start.3 = (f32[34,1,128]{2,0,1:T(8,128)}, f32[34,1,128]{2,0,1:T(8,128)S(1)}, u32[]{:S(2)}, u32[]{:S(2)}) collective-permute-start(f32[34,1,128]{2,0,1:T(8,128)} %get-tuple-element.40), channel_id=1, source_target_pairs={{1,0},{2,1},{3,2},{0,3},{5,4},{6,5},{7,6},{4,7},{9,8},{10,9},{11,1... | collective-permute-start | bytes 52232 | tf_op jit(solution)/shard_map/ppermute | solution.py:23
  38.8 17.1 %collective-permute-start.2 = (f32[34,1,128]{2,0,1:T(8,128)S(1)}, f32[34,1,128]{2,0,1:T(8,128)S(1)}, u32[]{:S(2)}, u32[]{:S(2)}) collective-permute-start(f32[34,1,128]{2,0,1:T(8,128)S(1)} %get-tuple-element.39), channel_id=1, source_target_pairs={{0,1},{1,2},{2,3},{3,0},{4,5},{5,6},{6,7},{7,4},{8,9},{9,10},{10,1... | collective-permute-start | bytes 52232 | tf_op jit(solution)/shard_map/ppermute | solution.py:22
  38.8 53.5 %copy-start.25 = (pred[32]{0:T(512)(128)(4,1)}, pred[32]{0:T(512)(128)(4,1)S(1)}, u32[]{:S(2)}) copy-start(pred[32]{0:T(512)(128)(4,1)S(1)} %get-tuple-element.58) | copy-start | bytes 100
  38.8 53.5 %copy-start.27 = (pred[32]{0:T(512)(128)(4,1)}, pred[32]{0:T(512)(128)(4,1)S(1)}, u32[]{:S(2)}) copy-start(pred[32]{0:T(512)(128)(4,1)S(1)} %get-tuple-element.59) | copy-start | bytes 100
  38.8 17.1 %copy-start.30 = (f32[128]{0:T(128)S(1)}, f32[128]{0:T(128)}, u32[]{:S(2)}) copy-start(f32[128]{0:T(128)} %param.16) | copy-start | bytes 1540
  55.9 21.4 %copy-start.12 = (f32[34,1,128]{2,0,1:T(8,128)}, f32[34,1,128]{2,0,1:T(8,128)S(1)}, u32[]{:S(2)}) copy-start(f32[34,1,128]{2,0,1:T(8,128)S(1)} %collective-permute-done.3) | copy-start | bytes 52228
  55.9 21.4 %copy-start.14 = (f32[34,1,128]{2,0,1:T(8,128)}, f32[34,1,128]{2,0,1:T(8,128)S(1)}, u32[]{:S(2)}) copy-start(f32[34,1,128]{2,0,1:T(8,128)S(1)} %collective-permute-done.2) | copy-start | bytes 52228
  58.1 21.1 %collective-permute-start.5 = (f32[1,64,128]{2,0,1:T(1,128)}, f32[1,64,128]{2,0,1:T(1,128)S(1)}, u32[]{:S(2)}, u32[]{:S(2)}) collective-permute-start(f32[1,64,128]{2,0,1:T(1,128)} %get-tuple-element.50), channel_id=1, source_target_pairs={{4,0},{8,4},{12,8},{16,12},{20,16},{24,20},{28,24},{0,28},{5,1},{9... | collective-permute-start | bytes 98312 | tf_op jit(solution)/shard_map/ppermute | solution.py:23
  60.5 18.7 %collective-permute-start.4 = (f32[1,64,128]{2,0,1:T(1,128)}, f32[1,64,128]{2,0,1:T(1,128)}, u32[]{:S(2)}, u32[]{:S(2)}) collective-permute-start(f32[1,64,128]{2,0,1:T(1,128)} %get-tuple-element.49), channel_id=1, source_target_pairs={{0,4},{4,8},{8,12},{12,16},{16,20},{20,24},{24,28},{28,0},{1,5},{5... | collective-permute-start | bytes 98312 | tf_op jit(solution)/shard_map/ppermute | solution.py:22
  79.1 74.0 %all-reduce.4.cloned.1.call-start = ((), (), s32[]{:S(2)}) async-start(), calls=%async_computation.4 | async-start | bytes 163840 | tf_op jit(solution)/shard_map/psum | solution.py:92
  79.9 12.3 %collective-permute-start.7 = (f32[34,1,128]{2,0,1:T(8,128)S(1)}, f32[34,1,128]{2,0,1:T(8,128)}, u32[]{:S(2)}, u32[]{:S(2)}) collective-permute-start(f32[34,1,128]{2,0,1:T(8,128)S(1)} %get-tuple-element.38), channel_id=1, source_target_pairs={{1,0},{2,1},{3,2},{0,3},{5,4},{6,5},{7,6},{4,7},{9,8},{10,9},{11,1... | collective-permute-start | bytes 52232 | tf_op jit(solution)/shard_map/ppermute | solution.py:23
  83.5 8.7 %collective-permute-start.6 = (f32[34,1,128]{2,0,1:T(8,128)S(1)}, f32[34,1,128]{2,0,1:T(8,128)}, u32[]{:S(2)}, u32[]{:S(2)}) collective-permute-start(f32[34,1,128]{2,0,1:T(8,128)S(1)} %get-tuple-element.37), channel_id=1, source_target_pairs={{0,1},{1,2},{2,3},{3,0},{4,5},{5,6},{6,7},{7,4},{8,9},{9,10},{10,1... | collective-permute-start | bytes 52232 | tf_op jit(solution)/shard_map/ppermute | solution.py:22
  101.2 51.9 %copy-start.11 = (f32[8,1280]{1,0:T(8,128)S(1)}, f32[8,1280]{1,0:T(8,128)}, u32[]{:S(2)}) copy-start(f32[8,1280]{1,0:T(8,128)} %param.17) | copy-start | bytes 122884
  101.2 145.2 %reduce-scatter.6.cloned.1.call-start = ((), (), s32[]{:S(2)}) async-start(), calls=%async_computation.5 | async-start | bytes 204800 | tf_op jit(solution)/shard_map/reduce_scatter | solution.py:91
  167.9 12.3 %copy-start = (bf16[16384,128]{1,0:T(8,128)(2,1)S(1)}, bf16[16384,128]{1,0:T(8,128)(2,1)}, u32[]{:S(2)}) copy-start(bf16[16384,128]{1,0:T(8,128)(2,1)} %param.11) | copy-start | bytes 12582916
  191.7 15.1 %collective-permute-start.9 = (f32[1,64,128]{2,0,1:T(1,128)}, f32[1,64,128]{2,0,1:T(1,128)S(1)}, u32[]{:S(2)}, u32[]{:S(2)}) collective-permute-start(f32[1,64,128]{2,0,1:T(1,128)} %get-tuple-element.48), channel_id=1, source_target_pairs={{4,0},{8,4},{12,8},{16,12},{20,16},{24,20},{28,24},{0,28},{5,1},{9... | collective-permute-start | bytes 98312 | tf_op jit(solution)/shard_map/ppermute | solution.py:23
  191.7 15.1 %collective-permute-start.8 = (f32[1,64,128]{2,0,1:T(1,128)}, f32[1,64,128]{2,0,1:T(1,128)S(1)}, u32[]{:S(2)}, u32[]{:S(2)}) collective-permute-start(f32[1,64,128]{2,0,1:T(1,128)} %get-tuple-element.47), channel_id=1, source_target_pairs={{0,4},{4,8},{8,12},{12,16},{16,20},{20,24},{24,28},{28,0},{1,5},{5... | collective-permute-start | bytes 98312 | tf_op jit(solution)/shard_map/ppermute | solution.py:22
  208.3 17.4 %collective-permute-start.11 = (f32[34,1,128]{2,0,1:T(8,128)}, f32[34,1,128]{2,0,1:T(8,128)}, u32[]{:S(2)}, u32[]{:S(2)}) collective-permute-start(f32[34,1,128]{2,0,1:T(8,128)} %get-tuple-element.36), channel_id=1, source_target_pairs={{1,0},{2,1},{3,2},{0,3},{5,4},{6,5},{7,6},{4,7},{9,8},{10,9},{11,1... | collective-permute-start | bytes 52232 | tf_op jit(solution)/shard_map/ppermute | solution.py:23
  211.7 14.0 %copy-start.13 = (f32[34,1,128]{2,0,1:T(8,128)S(1)}, f32[34,1,128]{2,0,1:T(8,128)}, u32[]{:S(2)}) copy-start(f32[34,1,128]{2,0,1:T(8,128)} %copy-done.12) | copy-start | bytes 52228
  211.7 14.0 %copy-start.15 = (f32[34,1,128]{2,0,1:T(8,128)S(1)}, f32[34,1,128]{2,0,1:T(8,128)}, u32[]{:S(2)}) copy-start(f32[34,1,128]{2,0,1:T(8,128)} %copy-done.14) | copy-start | bytes 52228
  211.7 14.0 %copy-start.26 = (pred[32]{0:T(512)(128)(4,1)S(1)}, pred[32]{0:T(512)(128)(4,1)}, u32[]{:S(2)}) copy-start(pred[32]{0:T(512)(128)(4,1)} %copy-done.25) | copy-start | bytes 100
  211.7 14.0 %copy-start.28 = (pred[32]{0:T(512)(128)(4,1)S(1)}, pred[32]{0:T(512)(128)(4,1)}, u32[]{:S(2)}) copy-start(pred[32]{0:T(512)(128)(4,1)} %copy-done.27) | copy-start | bytes 100
  211.7 14.0 %copy-start.32 = (f32[128]{0:T(128)S(1)}, f32[128]{0:T(128)}, u32[]{:S(2)}) copy-start(f32[128]{0:T(128)} %param.16) | copy-start | bytes 1540
  211.8 13.9 %collective-permute-start.10 = (f32[34,1,128]{2,0,1:T(8,128)}, f32[34,1,128]{2,0,1:T(8,128)}, u32[]{:S(2)}, u32[]{:S(2)}) collective-permute-start(f32[34,1,128]{2,0,1:T(8,128)} %get-tuple-element.35), channel_id=1, source_target_pairs={{0,1},{1,2},{2,3},{3,0},{4,5},{5,6},{6,7},{7,4},{8,9},{9,10},{10,1... | collective-permute-start | bytes 52232 | tf_op jit(solution)/shard_map/ppermute | solution.py:22
  225.6 253.1 %reduce-scatter.8.cloned.1.call-start = ((), (), s32[]{:S(2)}) async-start(), calls=%async_computation.6 | async-start | bytes 204800 | tf_op jit(solution)/shard_map/reduce_scatter | solution.py:91
  363.0 21.1 %copy-start.10 = (f32[16384,20]{0,1:T(8,128)S(1)}, f32[16384,20]{0,1:T(8,128)}, u32[]{:S(2)}) copy-start(f32[16384,20]{0,1:T(8,128)} %fusion.51) | copy-start | bytes 3932164
  365.0 30.8 %copy-start.2 = (f32[32,64,128]{2,0,1:T(8,128)}, f32[32,64,128]{2,0,1:T(8,128)S(1)}, u32[]{:S(2)}) copy-start(f32[32,64,128]{2,0,1:T(8,128)S(1)} %multiply_add_fusion.1) | copy-start | bytes 3145732
  365.1 15.7 %collective-permute-start.13 = (f32[1,64,128]{2,0,1:T(1,128)S(1)}, f32[1,64,128]{2,0,1:T(1,128)S(1)}, u32[]{:S(2)}, u32[]{:S(2)}) collective-permute-start(f32[1,64,128]{2,0,1:T(1,128)S(1)} %get-tuple-element.46), channel_id=1, source_target_pairs={{4,0},{8,4},{12,8},{16,12},{20,16},{24,20},{28,24},{0,28},{5,1},{9... | collective-permute-start | bytes 98312 | tf_op jit(solution)/shard_map/ppermute | solution.py:23
  366.3 14.5 %collective-permute-start.12 = (f32[1,64,128]{2,0,1:T(1,128)S(1)}, f32[1,64,128]{2,0,1:T(1,128)S(1)}, u32[]{:S(2)}, u32[]{:S(2)}) collective-permute-start(f32[1,64,128]{2,0,1:T(1,128)S(1)} %get-tuple-element.45), channel_id=1, source_target_pairs={{0,4},{4,8},{8,12},{12,16},{16,20},{20,24},{24,28},{28,0},{1,5},{5... | collective-permute-start | bytes 98312 | tf_op jit(solution)/shard_map/ppermute | solution.py:22
  382.1 14.4 %collective-permute-start.15 = (f32[34,1,128]{2,0,1:T(8,128)}, f32[34,1,128]{2,0,1:T(8,128)}, u32[]{:S(2)}, u32[]{:S(2)}) collective-permute-start(f32[34,1,128]{2,0,1:T(8,128)} %get-tuple-element.34), channel_id=1, source_target_pairs={{1,0},{2,1},{3,2},{0,3},{5,4},{6,5},{7,6},{4,7},{9,8},{10,9},{11,1... | collective-permute-start | bytes 52232 | tf_op jit(solution)/shard_map/ppermute | solution.py:23
  383.7 12.8 %collective-permute-start.14 = (f32[34,1,128]{2,0,1:T(8,128)}, f32[34,1,128]{2,0,1:T(8,128)}, u32[]{:S(2)}, u32[]{:S(2)}) collective-permute-start(f32[34,1,128]{2,0,1:T(8,128)} %get-tuple-element.33), channel_id=1, source_target_pairs={{0,1},{1,2},{2,3},{3,0},{4,5},{5,6},{6,7},{7,4},{8,9},{9,10},{10,1... | collective-permute-start | bytes 52232 | tf_op jit(solution)/shard_map/ppermute | solution.py:22
  401.8 11.9 %copy-start.22 = (f32[16384]{0:T(1024)S(1)}, f32[16384]{0:T(1024)}, u32[]{:S(2)}) copy-start(f32[16384]{0:T(1024)} %fusion.38) | copy-start | bytes 196612
  401.8 12.0 %copy-start.1 = (bf16[16384,128]{1,0:T(8,128)(2,1)S(1)}, bf16[16384,128]{1,0:T(8,128)(2,1)}, u32[]{:S(2)}) copy-start(bf16[16384,128]{1,0:T(8,128)(2,1)} %param.11) | copy-start | bytes 12582916
  424.7 15.3 %collective-permute-start.17 = (f32[1,64,128]{2,0,1:T(1,128)S(1)}, f32[1,64,128]{2,0,1:T(1,128)S(1)}, u32[]{:S(2)}, u32[]{:S(2)}) collective-permute-start(f32[1,64,128]{2,0,1:T(1,128)S(1)} %get-tuple-element.44), channel_id=1, source_target_pairs={{4,0},{8,4},{12,8},{16,12},{20,16},{24,20},{28,24},{0,28},{5,1},{9... | collective-permute-start | bytes 98312 | tf_op jit(solution)/shard_map/ppermute | solution.py:23
  424.7 15.2 %collective-permute-start.16 = (f32[1,64,128]{2,0,1:T(1,128)S(1)}, f32[1,64,128]{2,0,1:T(1,128)S(1)}, u32[]{:S(2)}, u32[]{:S(2)}) collective-permute-start(f32[1,64,128]{2,0,1:T(1,128)S(1)} %get-tuple-element.43), channel_id=1, source_target_pairs={{0,4},{4,8},{8,12},{12,16},{16,20},{20,24},{24,28},{28,0},{1,5},{5... | collective-permute-start | bytes 98312 | tf_op jit(solution)/shard_map/ppermute | solution.py:22
  431.1 8.8 %copy-start.7 = (f32[32,64,128]{2,0,1:T(8,128)S(1)}, f32[32,64,128]{2,0,1:T(8,128)}, u32[]{:S(2)}) copy-start(f32[32,64,128]{2,0,1:T(8,128)} %copy-done.6) | copy-start | bytes 3145732
  440.6 17.4 %collective-permute-start.19 = (f32[34,1,128]{2,0,1:T(8,128)}, f32[34,1,128]{2,0,1:T(8,128)S(1)}, u32[]{:S(2)}, u32[]{:S(2)}) collective-permute-start(f32[34,1,128]{2,0,1:T(8,128)} %get-tuple-element.32), channel_id=1, source_target_pairs={{1,0},{2,1},{3,2},{0,3},{5,4},{6,5},{7,6},{4,7},{9,8},{10,9},{11,1... | collective-permute-start | bytes 52232 | tf_op jit(solution)/shard_map/ppermute | solution.py:23
  444.0 14.1 %copy-start.3 = (f32[32,64,128]{2,0,1:T(8,128)S(1)}, f32[32,64,128]{2,0,1:T(8,128)}, u32[]{:S(2)}) copy-start(f32[32,64,128]{2,0,1:T(8,128)} %copy-done.2) | copy-start | bytes 3145732
  444.0 14.1 %copy-start.29 = (pred[32]{0:T(512)(128)(4,1)S(1)}, pred[32]{0:T(512)(128)(4,1)}, u32[]{:S(2)}) copy-start(pred[32]{0:T(512)(128)(4,1)} %copy-done.27) | copy-start | bytes 100
  444.0 14.1 %copy-start.33 = (f32[128]{0:T(128)S(1)}, f32[128]{0:T(128)}, u32[]{:S(2)}) copy-start(f32[128]{0:T(128)} %param.16) | copy-start | bytes 1540
  444.0 99.3 %copy-start.17 = (f32[8,1280]{1,0:T(8,128)S(1)}, f32[8,1280]{1,0:T(8,128)}, u32[]{:S(2)}) copy-start(f32[8,1280]{1,0:T(8,128)} %get-tuple-element.27) | copy-start | bytes 122884
  444.0 14.0 %collective-permute-start.18 = (f32[34,1,128]{2,0,1:T(8,128)}, f32[34,1,128]{2,0,1:T(8,128)}, u32[]{:S(2)}, u32[]{:S(2)}) collective-permute-start(f32[34,1,128]{2,0,1:T(8,128)} %get-tuple-element.31), channel_id=1, source_target_pairs={{0,1},{1,2},{2,3},{3,0},{4,5},{5,6},{6,7},{7,4},{8,9},{9,10},{10,1... | collective-permute-start | bytes 52232 | tf_op jit(solution)/shard_map/ppermute | solution.py:22
  456.3 88.3 %copy-start.4 = (f32[32,64,128]{2,0,1:T(8,128)S(1)}, f32[32,64,128]{2,0,1:T(8,128)}, u32[]{:S(2)}) copy-start(f32[32,64,128]{2,0,1:T(8,128)} %get-tuple-element.28) | copy-start | bytes 3145732
  456.3 88.3 %copy-start.16 = (f32[34,1,128]{2,0,1:T(8,128)S(1)}, f32[34,1,128]{2,0,1:T(8,128)}, u32[]{:S(2)}) copy-start(f32[34,1,128]{2,0,1:T(8,128)} %copy-done.14) | copy-start | bytes 52228
  (14 other events, 59.7 us)
Sparse Core Ops, SparseCore 0:
  79.2 21.9 reduce-scatter.3
  104.3 48.7 all-reduce.3
  225.8 20.6 reduce-scatter.5
  458.2 20.4 reduce-scatter.7
where the time goes:
time: 613 us; the launch traced here: 604 us
  blocking collectives  236 us (38%)
  matrix products  131 us (21%)
  waiting for transfers between devices  71.1 us (12%)
  other arithmetic  58.5 us (10%)
  local copies, waits for them, and re-layouts  54.1 us (9%)
  between operations  28.4 us (5%)
  starting transfers between devices  25.2 us (4%)
    psum x3, blocking collectives, norms_of(): lax.psum((inner(state_res, state_res, bias_res, bias_pre), inner(state_re...  124 us
    psum x2, blocking collectives, to_owners(): return lax.psum(owned, 'swath')  47.2 us
    dot_general x3, matrix products, partial_table(): table = jnp.dot(spread, inner_hot, precision=highest)  40.8 us
    psum x1, waiting for transfers between devices, to_owners(): return lax.psum(owned, 'swath')  40.4 us
    psum x1, blocking collectives, body(): lax.psum(inner(dir_state, state_out, dir_bias, bias_out), ('swath', 'chan'))  37.5 us
    mul x3, local copies, waits for them, and re-layouts, partial_table(): terms[:, None, :] * block_hot.T[None, :, :]  34.6 us
    reduce_scatter x3, waiting for transfers between devices, to_owners(): lax.psum_scatter(partial_value, 'chan', scatter_dimension=1, tiled=True)  30.6 us
    all_gather x2, blocking collectives, body(): hessian_everything = lax.all_gather(dir_bias, 'chan', axis=1, tiled=True)  27.7 us
  transfers between devices with their start and end apart: 24, of which 4 were waited for; matrix products, arithmetic and copies ran while one was open for 25% of the time, Pallas kernels for 0%

commit v1 on v0

v1 whole, which is shorter than its diff:
```python
import functools
import jax
import jax.numpy as jnp
from jax import lax
from jax.experimental import pallas as pl
from jax.experimental.pallas import tpu as pltpu
from jax.sharding import PartitionSpec as P

LEV = 128
NPRED = 8
CH_BLOCK = 256
OBS_BLOCK = 128
LAT_DEV = 32
LON_DEV = 64
GROUP = 8
PAD = 8
SHRINK = 2.0 ** -16
F32 = jnp.float32
BF16 = jnp.bfloat16
VMEM = pl.BlockSpec(memory_space=pltpu.VMEM)
SMEM = pl.BlockSpec(memory_space=pltpu.SMEM)
NT = (((1,), (1,)), ((), ()))


def two_parts(value):
    high = value.astype(BF16)
    low = (value - high.astype(F32)).astype(BF16)
    return high, low


def dot(one, two, dims=(((1,), (0,)), ((), ()))):
    return lax.dot_general(one, two, dims, preferred_element_type=F32)


def channel_hot(channel):
    rows = lax.broadcasted_iota(jnp.int32, (CH_BLOCK, OBS_BLOCK), 0)
    cols = []
    for line in range(GROUP):
        inner = jnp.bitwise_and(channel[line : line + 1], CH_BLOCK - 1)
        cols.append(jnp.where(rows == inner, 1.0, 0.0).astype(BF16))
    return jnp.concatenate(cols, axis=1)


def flat_lines(value):
    return jnp.concatenate([value[line : line + 1] for line in range(GROUP)], axis=1)


def spread(terms, block_row, blocks):
    high, low = two_parts(terms)
    pieces = jnp.concatenate([high, low], axis=0)
    wide = jnp.broadcast_to(block_row, pieces.shape)
    zero = jnp.zeros_like(pieces)
    return jnp.concatenate(
        [jnp.where(wide == float(b), pieces, zero) for b in range(blocks)], axis=0
    )


def put_table(out_ref, acc_ref, blocks, added):
    for b in range(blocks):
        at = slice(b * CH_BLOCK, (b + 1) * CH_BLOCK)
        low = 2 * NPRED * b
        total = acc_ref[low : low + NPRED] + acc_ref[low + NPRED : low + 2 * NPRED]
        out_ref[:, at] = total + added(at)


def first_bias_kernel(
    count_ref, innov_ref, prec_ref, chan_ref, pred_ref, prior_ref,
    source_ref, weight_ref, table_ref, diag_ref, acc_ref, dacc_ref,
):
    lines = innov_ref.shape[0]
    blocks = acc_ref.shape[0] // (2 * NPRED)
    acc_ref[...] = jnp.zeros_like(acc_ref)
    dacc_ref[...] = jnp.zeros_like(dacc_ref)

    def step(i, _):
        at = pl.ds(pl.multiple_of(i * GROUP, GROUP), GROUP)
        wide = pl.ds(pl.multiple_of(i * GROUP * OBS_BLOCK, GROUP * OBS_BLOCK), GROUP * OBS_BLOCK)
        slot = (
            (i * GROUP + lax.broadcasted_iota(jnp.int32, (GROUP, OBS_BLOCK), 0)) * OBS_BLOCK
            + lax.broadcasted_iota(jnp.int32, (GROUP, OBS_BLOCK), 1)
        )
        weight = jnp.where(slot < count_ref[0, 0], prec_ref[at], 0.0)
        source = weight * innov_ref[at]
        weight_ref[at] = weight
        source_ref[at] = source
        channel = chan_ref[at]
        hot = channel_hot(channel)
        block_row = flat_lines(lax.shift_right_logical(channel, 8).astype(F32)).astype(BF16)
        pred = pred_ref[:, wide]
        acc_ref[...] += dot(spread(pred * flat_lines(source), block_row, blocks), hot, NT)
        dacc_ref[...] += dot(spread(pred * pred * flat_lines(weight), block_row, blocks), hot, NT)
        return 0

    lax.fori_loop(0, lines // GROUP, step, 0)
    put_table(table_ref, acc_ref, blocks, lambda at: 0.0)
    put_table(diag_ref, dacc_ref, blocks, lambda at: prior_ref[:, at])


def bias_kernel(
    image_ref, weight_ref, chan_ref, pred_ref, coef_ref, prior_ref,
    value_ref, table_ref, acc_ref, look_ref,
):
    lines = image_ref.shape[0]
    blocks = acc_ref.shape[0] // (2 * NPRED)
    acc_ref[...] = jnp.zeros_like(acc_ref)
    for b in range(blocks):
        high, low = two_parts(coef_ref[:, b * CH_BLOCK : (b + 1) * CH_BLOCK])
        look_ref[2 * NPRED * b : 2 * NPRED * (b + 1)] = jnp.concatenate([high, low], axis=0)

    def step(i, _):
        at = pl.ds(pl.multiple_of(i * GROUP, GROUP), GROUP)
        wide = pl.ds(pl.multiple_of(i * GROUP * OBS_BLOCK, GROUP * OBS_BLOCK), GROUP * OBS_BLOCK)
        channel = chan_ref[at]
        hot = channel_hot(channel)
        block_f32 = flat_lines(lax.shift_right_logical(channel, 8).astype(F32))
        pred = pred_ref[:, wide]
        found = dot(look_ref[...], hot)
        block_wide = jnp.broadcast_to(block_f32, pred.shape)
        picked = jnp.zeros_like(pred)
        for b in range(blocks):
            low = 2 * NPRED * b
            both = found[low : low + NPRED] + found[low + NPRED : low + 2 * NPRED]
            picked = jnp.where(block_wide == float(b), both, picked)
        looked = jnp.sum(picked * pred, axis=0, keepdims=True)
        value = flat_lines(weight_ref[at]) * (flat_lines(image_ref[at]) + looked)
        value_ref[at] = jnp.concatenate(
            [value[:, j * OBS_BLOCK : (j + 1) * OBS_BLOCK] for j in range(GROUP)], axis=0
        )
        acc_ref[...] += dot(spread(pred * value, block_f32.astype(BF16), blocks), hot, NT)
        return 0

    lax.fori_loop(0, lines // GROUP, step, 0)
    put_table(table_ref, acc_ref, blocks, lambda at: prior_ref[:, at] * coef_ref[:, at])


def adjoint_kernel(scale, has_base, row_ref, value_ref, col_ref, jac_ref, *rest):
    if has_base:
        base_ref, out_ref = rest
        out_ref[...] = base_ref[...]
    else:
        (out_ref,) = rest
        out_ref[...] = jnp.zeros_like(out_ref)
    lines = value_ref.shape[0]
    cells = lax.broadcasted_iota(jnp.int32, (LON_DEV, OBS_BLOCK), 0)

    def step(i, _):
        at = pl.ds(pl.multiple_of(i * GROUP, GROUP), GROUP)
        value = value_ref[at]
        high = value.astype(BF16).astype(F32)
        low = value - high
        col = jnp.bitwise_and(col_ref[at], LON_DEV - 1)
        for j in range(GROUP):
            hit = cells == col[j : j + 1]
            left = jnp.concatenate(
                [jnp.where(hit, high[j : j + 1], 0.0), jnp.where(hit, low[j : j + 1], 0.0)], axis=0
            ).astype(BF16)
            line = i * GROUP + j
            jac = jac_ref[pl.ds(pl.multiple_of(line * OBS_BLOCK, OBS_BLOCK), OBS_BLOCK), :]
            got = dot(left, jac)
            row = row_ref[line]
            out_ref[row] += got[:LON_DEV] + got[LON_DEV:]
        return 0

    lax.fori_loop(0, lines // GROUP, step, 0)
    if scale != 1.0:
        out_ref[...] = out_ref[...] * scale


def fill_padded(pad_ref, g_ref, up_ref, down_ref, west_ref, east_ref, width):
    rows = g_ref.shape[0]
    pad_ref[width : width + rows, PAD : PAD + LON_DEV] = g_ref[...]
    pad_ref[0:width, PAD : PAD + LON_DEV] = up_ref[...]
    pad_ref[width + rows : 2 * width + rows, PAD : PAD + LON_DEV] = down_ref[...]
    pad_ref[:, PAD - width : PAD] = west_ref[...]
    pad_ref[:, PAD + LON_DEV : PAD + LON_DEV + width] = east_ref[...]


def smoothed_row(pad_ref, row, smooth):
    here = pad_ref[row]
    size = here.shape[0]
    beside = (
        pad_ref[row - 1]
        + pad_ref[row + 1]
        + pltpu.roll(here, 1, 0)
        + pltpu.roll(here, size - 1, 0)
    )
    return here + smooth * (beside - 4.0 * here)


def forward_kernel(
    row_ref, keep_ref, smooth_ref, g_ref, up_ref, down_ref, west_ref, east_ref, col_ref, jac_ref,
    image_ref, z_ref, pad_ref, zpad_ref, part_ref,
):
    rows = g_ref.shape[0]
    lines = col_ref.shape[0]
    smooth = smooth_ref[...]
    fill_padded(pad_ref, g_ref, up_ref, down_ref, west_ref, east_ref, 2)

    def first(r, _):
        zpad_ref[r] = smoothed_row(pad_ref, r + 1, smooth)
        return 0

    lax.fori_loop(0, rows + 2, first, 0)

    @pl.when(keep_ref[0] == 0)
    def _():
        zpad_ref[0] = jnp.zeros_like(zpad_ref[0])

    @pl.when(keep_ref[1] == 0)
    def _():
        zpad_ref[rows + 1] = jnp.zeros_like(zpad_ref[0])

    z_ref[...] = zpad_ref[1 : rows + 1, PAD : PAD + LON_DEV]

    def second(r, _):
        high, low = two_parts(smoothed_row(zpad_ref, r + 1, smooth)[PAD : PAD + LON_DEV])
        part_ref[r] = jnp.concatenate([high, low], axis=0)
        return 0

    lax.fori_loop(0, rows, second, 0)
    cells = lax.broadcasted_iota(jnp.int32, (LON_DEV, OBS_BLOCK), 0)

    def step(i, _):
        at = pl.ds(pl.multiple_of(i * GROUP, GROUP), GROUP)
        col = jnp.bitwise_and(col_ref[at], LON_DEV - 1)
        found = []
        for j in range(GROUP):
            line = i * GROUP + j
            jac = jac_ref[pl.ds(pl.multiple_of(line * OBS_BLOCK, OBS_BLOCK), OBS_BLOCK), :]
            got = dot(part_ref[row_ref[line]], jac, NT)
            both = got[:LON_DEV] + got[LON_DEV:]
            found.append(
                jnp.sum(jnp.where(cells == col[j : j + 1], both, 0.0), axis=0, keepdims=True)
            )
        image_ref[at] = jnp.concatenate(found, axis=0)
        return 0

    lax.fori_loop(0, lines // GROUP, step, 0)


def gram_kernel(
    lead_ref, smooth_ref, g_ref, up_ref, down_ref, west_ref, east_ref, z_ref, w_ref,
    rb_ref, zb_ref, wb_ref, ub_ref, vb_ref, sum_ref, pad_ref,
):
    rows = g_ref.shape[0]
    smooth = smooth_ref[...]
    fill_padded(pad_ref, g_ref, up_ref, down_ref, west_ref, east_ref, 1)

    def step(r, sums):
        z = z_ref[r]
        w = w_ref[r]
        v = smoothed_row(pad_ref, r + 1, smooth)[PAD : PAD + LON_DEV]
        made = []
        for total, (one, two) in zip(sums, ((z, z), (z, w), (w, w), (z, v), (w, v), (v, v))):
            made.append(total + jnp.sum((one * two).reshape(LON_DEV // 8, 8, LEV), axis=0))
        return tuple(made)

    zero = jnp.zeros((8, LEV), F32)
    zz, zw, ww, zv, wv, vv = lax.fori_loop(0, rows, step, (zero,) * 6)
    lead = jnp.where(lead_ref[0] > 0, 1.0, 0.0)
    rb, zb, wb, ub, vb = (ref[...] for ref in (rb_ref, zb_ref, wb_ref, ub_ref, vb_ref))

    def both(state, one, two):
        a = jnp.sum(state, axis=0, keepdims=True)
        b = jnp.sum(jnp.sum(one * two, axis=0, keepdims=True), axis=1, keepdims=True) * lead
        return a + b * (1.0 / LEV)

    sums = [
        both(zz, rb, rb), both(zz, rb, zb), both(zw, zb, wb), both(zw, rb, wb),
        both(ww, wb, ub), both(ww, wb, wb), both(wv, ub, vb), both(zv, rb, vb),
        both(wv, wb, vb), both(vv, vb, vb),
    ]
    sums += [jnp.zeros_like(sums[0])] * (16 - len(sums))
    sum_ref[...] = jnp.concatenate(sums, axis=0)


def final_kernel(count, *refs):
    ins = refs[:count]
    z_ref, w_ref, zb_ref, ub_ref, x_ref, xb_ref, norm_ref = refs[count:]
    total = ins[0][...]
    for ref in ins[1:]:
        total = total + ref[...]
    total = jnp.sum(total, axis=1, keepdims=True)
    rr, rz, zw, rw, wu, ww, uv, rv, wv, vv = (total[i : i + 1] for i in range(10))
    grow = 1.0 / SHRINK
    first = rz / (zw * grow)
    big = first * grow
    rz_one = rz - 2.0 * big * zw + big * big * wu
    rr_one = rr - 2.0 * big * rw + big * big * ww
    ratio = rz_one / rz
    lift = 1.0 + ratio
    curve = lift * lift * (zw * grow) - 2.0 * lift * first * wu * (grow * grow) + big * big * uv
    second = rz_one / curve
    main = first + second * lift
    side = first * second * grow
    main_big = main * grow
    rr_two = (
        rr + main_big * main_big * ww + side * side * vv
        - 2.0 * main_big * rw + 2.0 * side * rv - 2.0 * main_big * side * wv
    )
    x_ref[...] = main[:, None] * z_ref[...] - side[:, None] * w_ref[...]
    xb_ref[...] = main * zb_ref[...] - side * ub_ref[...]
    lane = lax.broadcasted_iota(jnp.int32, (8, LEV), 1)
    squares = jnp.where(lane == 0, rr, jnp.where(lane == 1, rr_one, rr_two))
    norm_ref[...] = jnp.sqrt(jnp.maximum(squares, 0.0))


def call(kernel, outs, scratch=(), flops=0, spaces=None, count=None, name=None):
    shapes = [jax.ShapeDtypeStruct(s, d) for s, d in outs]

    def run(*args):
        specs = [SMEM if i in (spaces or ()) else VMEM for i in range(len(args))]
        return pl.pallas_call(
            kernel,
            out_shape=shapes,
            in_specs=specs,
            out_specs=[VMEM] * len(shapes),
            scratch_shapes=list(scratch),
            cost_estimate=pl.CostEstimate(flops=flops, transcendentals=0, bytes_accessed=1 << 20),
            name=name,
            compiler_params=pltpu.CompilerParams(vmem_limit_bytes=48 << 20),
        )(*args)

    return run


def trade(value, axis, mask):
    size = lax.axis_size(axis)
    return lax.ppermute(value, axis, [(i, i ^ mask) for i in range(size)])


def scatter_rows(tables):
    size = lax.axis_size("swath")
    index = lax.axis_index("swath")
    table = jnp.concatenate(tables, axis=0)
    half = table.shape[1] // 2
    odd = index % 2
    mine = lax.dynamic_slice_in_dim(table, odd * half, half, 1)
    other = lax.dynamic_slice_in_dim(table, (1 - odd) * half, half, 1)
    mine = mine + trade(other, "swath", 1)
    place = index // 2
    width = half // (size // 2)
    own = lax.dynamic_slice_in_dim(mine, place * width, width, 1)
    got = [
        trade(lax.dynamic_slice_in_dim(mine, (place ^ m) * width, width, 1), "swath", 2 * m)
        for m in range(1, size // 2)
    ]
    for piece in got:
        own = own + piece
    return own


def sum_sectors(own):
    got = [trade(own, "chan", m) for m in range(1, lax.axis_size("chan"))]
    for piece in got:
        own = own + piece
    return own


def gather_rows(own):
    size = lax.axis_size("swath")
    index = lax.axis_index("swath")
    place = index // 2
    odd = index % 2
    width = own.shape[1]
    mine = jnp.zeros((own.shape[0], width * (size // 2)), own.dtype)
    mine = lax.dynamic_update_slice_in_dim(mine, own, place * width, 1)
    got = [trade(own, "swath", 2 * m) for m in range(1, size // 2)]
    for m, piece in enumerate(got, 1):
        mine = lax.dynamic_update_slice_in_dim(mine, piece, (place ^ m) * width, 1)
    other = trade(mine, "swath", 1)
    low = jnp.where(odd == 0, mine, other)
    high = jnp.where(odd == 0, other, mine)
    return jnp.concatenate([low, high], axis=1)


def halos(g, width):
    rows, cols = g.shape[0], g.shape[1]
    bands = lax.axis_size("swath")
    sectors = lax.axis_size("chan")
    up = lax.ppermute(g[rows - width :], "swath", [(i, i + 1) for i in range(bands - 1)])
    down = lax.ppermute(g[:width], "swath", [(i + 1, i) for i in range(bands - 1)])
    tall = lambda cut: jnp.concatenate([up[:, cut], g[:, cut], down[:, cut]], axis=0)
    west = lax.ppermute(
        tall(slice(cols - width, cols)), "chan", [(i, (i + 1) % sectors) for i in range(sectors)]
    )
    east = lax.ppermute(
        tall(slice(0, width)), "chan", [((i + 1) % sectors, i) for i in range(sectors)]
    )
    return up, down, west, east


def body(
    innovations, obs_precision, jacobian, predictors, obs_column, obs_channel, obs_count,
    smoothing, bias_precision,
):
    slots = obs_precision.shape[0]
    lines = slots // OBS_BLOCK
    owned = bias_precision.shape[1]
    channels = owned * lax.axis_size("chan")
    blocks = channels // CH_BLOCK
    band = lax.axis_index("swath")
    sector = lax.axis_index("chan")
    keep = jnp.stack([band > 0, band < lax.axis_size("swath") - 1]).astype(jnp.int32)
    lead = (sector == 0).astype(jnp.int32).reshape(1)
    smooth = smoothing.reshape(1, LEV)
    by_line = (lines, OBS_BLOCK)
    col = obs_column.reshape(by_line)
    channel = obs_channel.reshape(by_line)
    rows = col[:, 0] // LON_DEV
    prior = lax.dynamic_update_slice_in_dim(
        jnp.zeros((NPRED, channels), F32),
        jnp.where(band == 0, bias_precision, 0.0),
        sector * owned,
        1,
    )
    tile = (LAT_DEV, LON_DEV, LEV)
    table = (NPRED, channels)
    wide = LON_DEV + 2 * PAD
    acc = pltpu.VMEM((2 * NPRED * blocks, CH_BLOCK), F32)
    hot_flops = 2 * 2 * NPRED * blocks * CH_BLOCK * slots
    tile_flops = 4 * LON_DEV * LEV * slots
    line_out = (by_line, F32)

    first_bias = call(
        first_bias_kernel, [line_out, line_out, (table, F32), (table, F32)], [acc, acc],
        2 * hot_flops, (0,), name="first_bias",
    )
    bias = call(
        bias_kernel, [line_out, (table, F32)],
        [acc, pltpu.VMEM((2 * NPRED * blocks, CH_BLOCK), BF16)], 2 * hot_flops, name="bias",
    )

    def adjoint(value, base, scale):
        kernel = functools.partial(adjoint_kernel, scale, base is not None)
        args = (rows, value, col, jacobian) + (() if base is None else (base,))
        return call(kernel, [(tile, F32)], (), tile_flops, (0,), name="adjoint")(*args)[0]

    forward = call(
        forward_kernel, [line_out, (tile, F32)],
        [
            pltpu.VMEM((LAT_DEV + 4, wide, LEV), F32),
            pltpu.VMEM((LAT_DEV + 2, wide, LEV), F32),
            pltpu.VMEM((LAT_DEV, 2 * LON_DEV, LEV), BF16),
        ],
        tile_flops, (0, 1), name="forward",
    )
    gram = call(
        gram_kernel, [((16, LEV), F32)], [pltpu.VMEM((LAT_DEV + 2, wide, LEV), F32)],
        1 << 22, (0,), name="gram",
    )

    source, weight, table0, diag0 = first_bias(
        obs_count, innovations.reshape(by_line), obs_precision.reshape(by_line), channel,
        predictors, prior,
    )
    both = scatter_rows([table0, diag0])
    g0 = adjoint(source, None, 1.0)
    both = sum_sectors(both)
    rb, diag = both[:NPRED], both[NPRED:]
    zb = rb / diag
    z_all = gather_rows(zb)
    image, z = forward(rows, keep, smooth, g0, *halos(g0, 2), col, jacobian)
    value, table1 = bias(image, weight, channel, predictors, z_all, prior)
    wb = scatter_rows([table1])
    g1 = adjoint(value, g0, SHRINK)
    wb = sum_sectors(wb) * SHRINK
    ub = wb / diag
    u_all = gather_rows(ub)
    image, w = forward(rows, keep, smooth, g1, *halos(g1, 2), col, jacobian)
    value, table2 = bias(image, weight, channel, predictors, u_all, prior)
    vb = scatter_rows([table2])
    g2 = adjoint(value, g1, 1.0)
    vb = sum_sectors(vb)
    sums = gram(lead, smooth, g2, *halos(g2, 1), z, w, rb, zb, wb, ub, vb)[0]
    sums = sums + trade(sums, "swath", 1)
    got = [trade(sums, "swath", 2 * m) for m in range(1, lax.axis_size("swath") // 2)]
    for piece in got:
        sums = sums + piece
    got = [sums] + [trade(sums, "chan", m) for m in range(1, lax.axis_size("chan"))]
    own_z = lax.dynamic_slice_in_dim(z_all, sector * owned, owned, 1)
    own_u = lax.dynamic_slice_in_dim(u_all, sector * owned, owned, 1)
    x, xb, norms = call(
        functools.partial(final_kernel, len(got)),
        [(tile, F32), ((NPRED, owned), F32), ((8, LEV), F32)], name="final",
    )(*got, z, w, own_z, own_u)
    return x, xb, norms[0, :3]


def solution(mesh):
    placed = (
        P(("swath", "chan")),
        P(("swath", "chan")),
        P(("swath", "chan"), None),
        P(None, ("swath", "chan")),
        P(("swath", "chan")),
        P(("swath", "chan")),
        P("swath", "chan"),
        P(),
        P(None, "chan"),
    )
    return jax.shard_map(
        body,
        mesh=mesh,
        in_specs=placed,
        out_specs=(P("swath", "chan", None), P(None, "chan"), P()),
        check_vma=False,
    )
```

time: 613 us -> 191 us (0.31); the launches traced: 604 us -> 190 us
  blocking collectives: 236 us -> 0 us
  matrix products: 131 us -> 0 us
  Pallas kernels: 0 us -> 69.6 us
  other arithmetic: 58.5 us -> 3.67 us
  starting transfers between devices: 25.2 us -> 70.1 us
  waiting for transfers between devices: 71.1 us -> 28.6 us
  local copies, waits for them, and re-layouts: 54.1 us -> 15.5 us
  between operations: 28.4 us -> 2.09 us
    psum x6 -> x0, blocking collectives: 208 us -> none  [the longest x3 124 us: norms_of(): lax.psum((inner(state_res, state_res, bias_res, bias_pre), inner(state_re...]
    dot_general x15 -> x0, matrix products: 131 us -> none  [the longest x3 40.8 us: partial_table(): table = jnp.dot(spread, inner_hot, precision=highest)]
    pallas_call x0 -> x10, Pallas kernels: none -> 69.6 us  [run(): pl.pallas_call(kernel, out_shape=shapes, in_specs=specs, out_specs=[VMEM]...]
    ppermute x20 -> x48, starting transfers between devices: 25 us -> 70.1 us  [the longest x36 47.4 us: trade(): return lax.ppermute(value, axis, [(i, i ^ mask) for i in range(size)])]
    psum x1 -> x0, waiting for transfers between devices: 40.4 us -> none  [to_owners(): return lax.psum(owned, 'swath')]
    mul x3 -> x0, local copies, waits for them, and re-layouts: 34.6 us -> none  [partial_table(): terms[:, None, :] * block_hot.T[None, :, :]]
    reduce_scatter x3 -> x0, waiting for transfers between devices: 30.6 us -> none  [to_owners(): lax.psum_scatter(partial_value, 'chan', scatter_dimension=1, tiled=True)]
    ppermute x20 -> x48, waiting for transfers between devices: 0.05 us -> 28.6 us  [the longest x36 26.1 us: trade(): return lax.ppermute(value, axis, [(i, i ^ mask) for i in range(size)])]
  transfers between devices with their start and end apart: 24 -> 48, of which waited for: 4 -> 22; matrix products, arithmetic and copies ran while one was open for 25% -> 2% of each run, Pallas kernels for 0% -> 11%
where the time goes in v1:
time: 191 us; the launch traced here: 190 us
  starting transfers between devices  70.1 us (37%)
  Pallas kernels  69.6 us (36%)
  waiting for transfers between devices  28.6 us (15%)
  local copies, waits for them, and re-layouts  15.5 us (8%)
  other arithmetic  3.67 us (2%)
  between operations  2.09 us (1%)
    pallas_call x10, Pallas kernels, run(): pl.pallas_call(kernel, out_shape=shapes, in_specs=specs, out_specs=[VMEM]...  69.6 us
    ppermute x36, starting transfers between devices, trade(): return lax.ppermute(value, axis, [(i, i ^ mask) for i in range(size)])  47.4 us
    ppermute x36, waiting for transfers between devices, trade(): return lax.ppermute(value, axis, [(i, i ^ mask) for i in range(size)])  26.1 us
    unnamed x51, local copies, waits for them, and re-layouts  12.1 us
    ppermute x3, starting transfers between devices, halos(): lax.ppermute(tall(slice(0, width)), 'chan', [((i + 1) % sectors, i) for i...  9.42 us
    ppermute x3, starting transfers between devices, halos(): lax.ppermute(g[rows - width:], 'swath', [(i, i + 1) for i in range(bands...  7.37 us
    ppermute x3, starting transfers between devices, halos(): lax.ppermute(g[:width], 'swath', [(i + 1, i) for i in range(bands - 1)])  3.85 us
  transfers between devices with their start and end apart: 48, of which 22 were waited for; matrix products, arithmetic and copies ran while one was open for 2% of the time, Pallas kernels for 11%

profile of v1, /device:TPU:0, one launch (start us, length us, event | category | flops | bytes accessed | tf_op | source)
XLA Modules:
  0.0 189.5 jit_solution(13006979173264085658)
XLA Ops:
  5.7 8.8 %first_bias.1 = (f32[128,128]{1,0:T(8,128)S(1)}, f32[128,128]{1,0:T(8,128)S(1)}, f32[8,5120]{1,0:T(8,128)S(1)}, f32[8,5120]{1,0:T(8,128)S(1)}) custom-call(s32[1,1]{1,0:T(1,128)S(6)} %copy.22.count_ref, f32[128,128]{1,0:T(8,128)S(1)} %bitcast.19, f32[128,128]{1,0:T(8,128)S(1)} %bitcast.20, s32[128,128]{1,0:T(8,128)S(1)} %bitcast.21, ...), custom_call_target="tpu_custom_call" | custom-call | flops 5368709120 | bytes 1048576 | tf_op jit(solution)/shard_map/first_bias/pallas_call | solution.py:313
  14.8 2.2 %copy-done = bf16[16384,128]{1,0:T(8,128)(2,1)S(1)} copy-done((bf16[16384,128]{1,0:T(8,128)(2,1)S(1)}, bf16[16384,128]{1,0:T(8,128)(2,1)}, u32[]{:S(2)}) %copy-start) | copy-done | bytes 4194328
  17.0 4.2 %adjoint.3.g_ref.rest_0_ = f32[32,64,128]{2,1,0:T(8,128)S(1)} custom-call(s32[128]{0:T(128)S(1)} %and_select_fusion.row_ref, f32[128,128]{1,0:T(8,128)S(1)} %get-tuple-element.18.value_ref, s32[128,128]{1,0:T(8,128)S(1)} %bitcast.11, bf16[16384,128]{1,0:T(8,128)(2,1)S(1)} %copy-done), custom_call_target="tpu_custom_call" | custom-call | flops 536870912 | bytes 1048576 | tf_op jit(solution)/shard_map/adjoint/pallas_call | solution.py:313
  21.2 2.5 %collective-permute-start = (f32[2,64,128]{2,1,0:T(8,128)S(1)}, f32[2,64,128]{2,1,0:T(8,128)S(1)}, u32[]{:S(2)}, u32[]{:S(2)}) collective-permute-start(f32[2,64,128]{2,1,0:T(8,128)S(1)} %get-tuple-element.49), channel_id=1, source_target_pairs={{0,4},{4,8},{8,12},{12,16},{16,20},{20,24},{24,28},{1,5},{5,9},{9,... | collective-permute-start | bytes 196616 | tf_op jit(solution)/shard_map/ppermute | solution.py:381
  23.8 1.3 collective-permute-start.1
  25.3 4.1 %collective-permute-start.5 = (f32[16,640]{1,0:T(8,128)S(1)}, f32[16,640]{1,0:T(8,128)S(1)}, u32[]{:S(2)}, u32[]{:S(2)}) collective-permute-start(f32[16,640]{1,0:T(8,128)S(1)} %get-tuple-element.54), channel_id=1, source_target_pairs={{0,8},{4,12},{8,0},{12,4},{16,24},{20,28},{24,16},{28,20},{1,9},{5... | collective-permute-start | bytes 122888 | tf_op jit(solution)/shard_map/ppermute | solution.py:329
  29.4 1.5 collective-permute-start.6
  32.0 1.9 collective-permute-done.6
  33.8 2.0 %collective-permute-done.7 = f32[16,640]{1,0:T(8,128)S(1)} collective-permute-done((f32[16,640]{1,0:T(8,128)S(1)}, f32[16,640]{1,0:T(8,128)S(1)}, u32[]{:S(2)}, u32[]{:S(2)}) %collective-permute-start.7) | collective-permute-done | bytes 40992 | tf_op jit(solution)/shard_map/ppermute | solution.py:329
  35.8 3.7 %collective-permute-start.10 = (f32[16,640]{1,0:T(8,128)S(1)}, f32[16,640]{1,0:T(8,128)S(1)}, u32[]{:S(2)}, u32[]{:S(2)}) collective-permute-start(f32[16,640]{1,0:T(8,128)S(1)} %add_add_fusion.1), channel_id=1, source_target_pairs={{0,3},{1,2},{2,1},{3,0},{4,7},{5,6},{6,5},{7,4},{8,11},{9,10},{10,... | collective-permute-start | bytes 122888 | tf_op jit(solution)/shard_map/ppermute | solution.py:329
  40.3 3.7 %collective-permute-start.3 = (f32[36,2,128]{2,1,0:T(2,128)S(1)}, f32[36,2,128]{2,1,0:T(2,128)S(1)}, u32[]{:S(2)}, u32[]{:S(2)}) collective-permute-start(f32[36,2,128]{2,1,0:T(2,128)S(1)} %pad_maximum_fusion.3), channel_id=1, source_target_pairs={{1,0},{2,1},{3,2},{0,3},{5,4},{6,5},{7,6},{4,7},{9,8},{10,9},{11,1... | collective-permute-start | bytes 110600 | tf_op jit(solution)/shard_map/ppermute | solution.py:387
  44.6 1.5 collective-permute-start.11
  46.1 2.0 %collective-permute-start.2 = (f32[36,2,128]{2,1,0:T(2,128)S(1)}, f32[36,2,128]{2,1,0:T(2,128)S(1)}, u32[]{:S(2)}, u32[]{:S(2)}) collective-permute-start(f32[36,2,128]{2,1,0:T(2,128)S(1)} %pad_maximum_fusion.2), channel_id=1, source_target_pairs={{0,1},{1,2},{2,3},{3,0},{4,5},{5,6},{6,7},{7,4},{8,9},{9,10},{10,1... | collective-permute-start | bytes 110600 | tf_op jit(solution)/shard_map/ppermute | solution.py:384
  48.1 2.0 %collective-permute-start.13 = (f32[8,640]{1,0:T(8,128)S(1)}, f32[8,640]{1,0:T(8,128)S(1)}, u32[]{:S(2)}, u32[]{:S(2)}) collective-permute-start(f32[8,640]{1,0:T(8,128)S(1)} %get-tuple-element.37.zb_ref), channel_id=1, source_target_pairs={{0,24},{4,28},{8,16},{12,20},{16,8},{20,12},{24,0},{28,4},{1,25},{... | collective-permute-start | bytes 61448 | tf_op jit(solution)/shard_map/ppermute | solution.py:329
  50.1 1.7 collective-permute-done.12
  52.9 8.8 %forward.2 = (f32[128,128]{1,0:T(8,128)S(1)}, f32[32,64,128]{2,1,0:T(8,128)S(1)}) custom-call(s32[128]{0:T(128)S(1)} %and_select_fusion.row_ref, s32[2]{0:T(128)S(1)} %add_convert_fusion.keep_ref, f32[1,128]{1,0:T(1,128)S(1)} %bitcast.16, f32[32,64,128]{2,1,0:T(8,128)S(1)} %adjoint.3.g_ref.rest_0_, f32[2,64,128]{2,1,0:T(8,128)S(1)} %collective-permute-done.up_ref, ...), custom_call_target="tpu_custom_call" | custom-call | flops 536870912 | bytes 1048576 | tf_op jit(solution)/shard_map/forward/pallas_call | solution.py:313
  62.6 12.3 %bias.2 = (f32[128,128]{1,0:T(8,128)S(1)}, f32[8,5120]{1,0:T(8,128)S(1)}) custom-call(f32[128,128]{1,0:T(8,128)S(1)} %get-tuple-element.19.image_ref, f32[128,128]{1,0:T(8,128)S(1)} %get-tuple-element.20.weight_ref, s32[128,128]{1,0:T(8,128)S(1)} %bitcast.22, f32[8,16384]{1,0:T(8,128)S(1)} %copy-done.10, f32[8,5120]{1,0:T(8,128)S(1)} %pad_maximum_fusion.coef_ref, ...), custom_call_target="tpu_custom_call" | custom-call | flops 5368709120 | bytes 1048576 | tf_op jit(solution)/shard_map/bias/pallas_call | solution.py:313
  75.0 5.9 %adjoint.4.g_ref.rest_0_ = f32[32,64,128]{2,1,0:T(8,128)S(1)} custom-call(s32[128]{0:T(128)S(1)} %and_select_fusion.row_ref, f32[128,128]{1,0:T(8,128)S(1)} %get-tuple-element.23.value_ref, s32[128,128]{1,0:T(8,128)S(1)} %bitcast.13, bf16[16384,128]{1,0:T(8,128)(2,1)} %jac_ref.9, f32[32,64,128]{2,1,0:T(8,128)S(1)} %adjoint.3.g_ref.rest_0_), custom_call_target="tpu_custom_call" | custom-call | flops 536870912 | bytes 1048576 | tf_op jit(solution)/shard_map/adjoint/pallas_call | solution.py:313
  80.9 2.4 %collective-permute-start.15 = (f32[2,64,128]{2,1,0:T(8,128)S(1)}, f32[2,64,128]{2,1,0:T(8,128)S(1)}, u32[]{:S(2)}, u32[]{:S(2)}) collective-permute-start(f32[2,64,128]{2,1,0:T(8,128)S(1)} %get-tuple-element.45), channel_id=1, source_target_pairs={{0,4},{4,8},{8,12},{12,16},{16,20},{20,24},{24,28},{1,5},{5,9},{9,... | collective-permute-start | bytes 196616 | tf_op jit(solution)/shard_map/ppermute | solution.py:381
  85.5 3.0 %collective-permute-start.20 = (f32[8,640]{1,0:T(8,128)S(1)}, f32[8,640]{1,0:T(8,128)S(1)}, u32[]{:S(2)}, u32[]{:S(2)}) collective-permute-start(f32[8,640]{1,0:T(8,128)S(1)} %get-tuple-element.60), channel_id=1, source_target_pairs={{0,8},{4,12},{8,0},{12,4},{16,24},{20,28},{24,16},{28,20},{1,9},{5... | collective-permute-start | bytes 61448 | tf_op jit(solution)/shard_map/ppermute | solution.py:329
  89.7 1.4 collective-permute-start.22
  92.3 2.0 %collective-permute-done.22 = f32[8,640]{1,0:T(8,128)S(1)} collective-permute-done((f32[8,640]{1,0:T(8,128)S(1)}, f32[8,640]{1,0:T(8,128)S(1)}, u32[]{:S(2)}, u32[]{:S(2)}) %collective-permute-start.22) | collective-permute-done | bytes 20512 | tf_op jit(solution)/shard_map/ppermute | solution.py:329
  94.5 2.4 %collective-permute-start.24 = (f32[8,640]{1,0:T(8,128)S(1)}, f32[8,640]{1,0:T(8,128)S(1)}, u32[]{:S(2)}, u32[]{:S(2)}) collective-permute-start(f32[8,640]{1,0:T(8,128)S(1)} %add_add_fusion.4), channel_id=1, source_target_pairs={{0,2},{1,3},{2,0},{3,1},{4,6},{5,7},{6,4},{7,5},{8,10},{9,11},{10,... | collective-permute-start | bytes 61448 | tf_op jit(solution)/shard_map/ppermute | solution.py:329
  96.9 1.9 %collective-permute-start.25 = (f32[8,640]{1,0:T(8,128)S(1)}, f32[8,640]{1,0:T(8,128)S(1)}, u32[]{:S(2)}, u32[]{:S(2)}) collective-permute-start(f32[8,640]{1,0:T(8,128)S(1)} %add_add_fusion.4), channel_id=1, source_target_pairs={{0,3},{1,2},{2,1},{3,0},{4,7},{5,6},{6,5},{7,4},{8,11},{9,10},{10,... | collective-permute-start | bytes 61448 | tf_op jit(solution)/shard_map/ppermute | solution.py:329
  98.9 2.0 %collective-permute-start.18 = (f32[36,2,128]{2,1,0:T(2,128)S(1)}, f32[36,2,128]{2,1,0:T(2,128)S(1)}, u32[]{:S(2)}, u32[]{:S(2)}) collective-permute-start(f32[36,2,128]{2,1,0:T(2,128)S(1)} %pad_maximum_fusion.5), channel_id=1, source_target_pairs={{1,0},{2,1},{3,2},{0,3},{5,4},{6,5},{7,6},{4,7},{9,8},{10,9},{11,1... | collective-permute-start | bytes 110600 | tf_op jit(solution)/shard_map/ppermute | solution.py:387
  100.8 1.7 collective-permute-done.25
  103.8 1.9 %collective-permute-start.26 = (f32[8,640]{1,0:T(8,128)S(1)}, f32[8,640]{1,0:T(8,128)S(1)}, u32[]{:S(2)}, u32[]{:S(2)}) collective-permute-start(f32[8,640]{1,0:T(8,128)S(1)} %get-tuple-element.34.ub_ref), channel_id=1, source_target_pairs={{0,8},{4,12},{8,0},{12,4},{16,24},{20,28},{24,16},{28,20},{1,9},{5... | collective-permute-start | bytes 61448 | tf_op jit(solution)/shard_map/ppermute | solution.py:329
  105.9 1.5 collective-permute-start.28
  108.2 1.5 collective-permute-done.27
  114.9 8.7 %forward.3 = (f32[128,128]{1,0:T(8,128)S(1)}, f32[32,64,128]{2,1,0:T(8,128)S(1)}) custom-call(s32[128]{0:T(128)S(1)} %and_select_fusion.row_ref, s32[2]{0:T(128)S(1)} %add_convert_fusion.keep_ref, f32[1,128]{1,0:T(1,128)S(1)} %bitcast.17, f32[32,64,128]{2,1,0:T(8,128)S(1)} %adjoint.4.g_ref.rest_0_, f32[2,64,128]{2,1,0:T(8,128)S(1)} %collective-permute-done.15.up_ref, ...), custom_call_target="tpu_custom_call" | custom-call | flops 536870912 | bytes 1048576 | tf_op jit(solution)/shard_map/forward/pallas_call | solution.py:313
  127.3 12.3 %bias.3 = (f32[128,128]{1,0:T(8,128)S(1)}, f32[8,5120]{1,0:T(8,128)S(1)}) custom-call(f32[128,128]{1,0:T(8,128)S(1)} %get-tuple-element.24.image_ref, f32[128,128]{1,0:T(8,128)S(1)} %copy-done.18, s32[128,128]{1,0:T(8,128)S(1)} %bitcast.23, f32[8,16384]{1,0:T(8,128)S(1)} %copy-done.11, f32[8,5120]{1,0:T(8,128)S(1)} %pad_maximum_fusion.1.coef_ref, ...), custom_call_target="tpu_custom_call" | custom-call | flops 5368709120 | bytes 1048576 | tf_op jit(solution)/shard_map/bias/pallas_call | solution.py:313
  139.7 5.9 %adjoint.5.g_ref = f32[32,64,128]{2,1,0:T(8,128)S(1)} custom-call(s32[128]{0:T(128)S(1)} %and_select_fusion.row_ref, f32[128,128]{1,0:T(8,128)S(1)} %get-tuple-element.26.value_ref, s32[128,128]{1,0:T(8,128)S(1)} %bitcast.15, bf16[16384,128]{1,0:T(8,128)(2,1)} %jac_ref.9, f32[32,64,128]{2,1,0:T(8,128)S(1)} %adjoint.4.g_ref.rest_0_), custom_call_target="tpu_custom_call" | custom-call | flops 536870912 | bytes 1048576 | tf_op jit(solution)/shard_map/adjoint/pallas_call | solution.py:313
  145.6 2.4 %collective-permute-start.30 = (f32[1,64,128]{2,1,0:T(8,128)S(1)}, f32[1,64,128]{2,1,0:T(8,128)S(1)}, u32[]{:S(2)}, u32[]{:S(2)}) collective-permute-start(f32[1,64,128]{2,1,0:T(8,128)S(1)} %get-tuple-element.41), channel_id=1, source_target_pairs={{0,4},{4,8},{8,12},{12,16},{16,20},{20,24},{24,28},{1,5},{5,9},{9,... | collective-permute-start | bytes 98312 | tf_op jit(solution)/shard_map/ppermute | solution.py:381
  149.9 1.8 collective-permute-done.31.down_ref
  151.7 3.0 %collective-permute-start.35 = (f32[8,640]{1,0:T(8,128)S(1)}, f32[8,640]{1,0:T(8,128)S(1)}, u32[]{:S(2)}, u32[]{:S(2)}) collective-permute-start(f32[8,640]{1,0:T(8,128)S(1)} %get-tuple-element.57), channel_id=1, source_target_pairs={{0,8},{4,12},{8,0},{12,4},{16,24},{20,28},{24,16},{28,20},{1,9},{5... | collective-permute-start | bytes 61448 | tf_op jit(solution)/shard_map/ppermute | solution.py:329
  155.9 1.4 collective-permute-start.37
  157.3 3.8 %collective-permute-start.33 = (f32[34,1,128]{2,1,0:T(1,128)S(1)}, f32[34,1,128]{2,1,0:T(1,128)S(1)}, u32[]{:S(2)}, u32[]{:S(2)}) collective-permute-start(f32[34,1,128]{2,1,0:T(1,128)S(1)} %pad_maximum_fusion.7), channel_id=1, source_target_pairs={{1,0},{2,1},{3,2},{0,3},{5,4},{6,5},{7,6},{4,7},{9,8},{10,9},{11,1... | collective-permute-start | bytes 52232 | tf_op jit(solution)/shard_map/ppermute | solution.py:387
  161.2 3.8 %collective-permute-start.39 = (f32[8,640]{1,0:T(8,128)S(1)}, f32[8,640]{1,0:T(8,128)S(1)}, u32[]{:S(2)}, u32[]{:S(2)}) collective-permute-start(f32[8,640]{1,0:T(8,128)S(1)} %add_add_fusion.3), channel_id=1, source_target_pairs={{0,2},{1,3},{2,0},{3,1},{4,6},{5,7},{6,4},{7,5},{8,10},{9,11},{10,... | collective-permute-start | bytes 61448 | tf_op jit(solution)/shard_map/ppermute | solution.py:329
  166.7 3.8 %collective-permute-done.40 = f32[8,640]{1,0:T(8,128)S(1)} collective-permute-done((f32[8,640]{1,0:T(8,128)S(1)}, f32[8,640]{1,0:T(8,128)S(1)}, u32[]{:S(2)}, u32[]{:S(2)}) %collective-permute-start.40) | collective-permute-done | bytes 20512 | tf_op jit(solution)/shard_map/ppermute | solution.py:329
  171.2 1.3 gram.1
  173.8 1.5 collective-permute-start.42
  175.9 1.4 collective-permute-start.44
  177.4 1.5 collective-permute-done.43
  178.9 1.5 collective-permute-done.44
  180.4 1.8 collective-permute-start.46
  182.2 2.6 %collective-permute-start.47 = (f32[16,128]{1,0:T(8,128)S(1)}, f32[16,128]{1,0:T(8,128)S(1)}, u32[]{:S(2)}, u32[]{:S(2)}) collective-permute-start(f32[16,128]{1,0:T(8,128)S(1)} %add_add_fusion.5.refs_0_), channel_id=1, source_target_pairs={{0,3},{1,2},{2,1},{3,0},{4,7},{5,6},{6,5},{7,4},{8,11},{9,10},{10,... | collective-permute-start | bytes 24584 | tf_op jit(solution)/shard_map/ppermute | solution.py:329
  185.0 2.6 %collective-permute-done.47.refs_3_ = f32[16,128]{1,0:T(8,128)S(1)} collective-permute-done((f32[16,128]{1,0:T(8,128)S(1)}, f32[16,128]{1,0:T(8,128)S(1)}, u32[]{:S(2)}, u32[]{:S(2)}) %collective-permute-start.47) | collective-permute-done | bytes 8224 | tf_op jit(solution)/shard_map/ppermute | solution.py:329
  187.7 1.3 final.1
  (166 shorter events, 33.2 us)
Async XLA Ops:
  14.6 10.6 %collective-permute-start.4 = (f32[16,2560]{1,0:T(8,128)S(1)}, f32[16,2560]{1,0:T(8,128)S(1)}, u32[]{:S(2)}, u32[]{:S(2)}) collective-permute-start(f32[16,2560]{1,0:T(8,128)S(1)} %constant_dynamic-slice_fusion.11), channel_id=1, source_target_pairs={{0,4},{4,0},{8,12},{12,8},{16,20},{20,16},{24,28},{28,24},{1,5},{5... | collective-permute-start | bytes 491528 | tf_op jit(solution)/shard_map/ppermute | solution.py:329
  21.2 3.9 %collective-permute-start = (f32[2,64,128]{2,1,0:T(8,128)S(1)}, f32[2,64,128]{2,1,0:T(8,128)S(1)}, u32[]{:S(2)}, u32[]{:S(2)}) collective-permute-start(f32[2,64,128]{2,1,0:T(8,128)S(1)} %get-tuple-element.49), channel_id=1, source_target_pairs={{0,4},{4,8},{8,12},{12,16},{16,20},{20,24},{24,28},{1,5},{5,9},{9,... | collective-permute-start | bytes 196616 | tf_op jit(solution)/shard_map/ppermute | solution.py:381
  23.8 8.0 %collective-permute-start.1 = (f32[2,64,128]{2,1,0:T(8,128)S(1)}, f32[2,64,128]{2,1,0:T(8,128)S(1)}, u32[]{:S(2)}, u32[]{:S(2)}) collective-permute-start(f32[2,64,128]{2,1,0:T(8,128)S(1)} %get-tuple-element.48), channel_id=1, source_target_pairs={{4,0},{8,4},{12,8},{16,12},{20,16},{24,20},{28,24},{5,1},{9,5},{13... | collective-permute-start | bytes 196616 | tf_op jit(solution)/shard_map/ppermute | solution.py:382
  25.3 6.7 %collective-permute-start.5 = (f32[16,640]{1,0:T(8,128)S(1)}, f32[16,640]{1,0:T(8,128)S(1)}, u32[]{:S(2)}, u32[]{:S(2)}) collective-permute-start(f32[16,640]{1,0:T(8,128)S(1)} %get-tuple-element.54), channel_id=1, source_target_pairs={{0,8},{4,12},{8,0},{12,4},{16,24},{20,28},{24,16},{28,20},{1,9},{5... | collective-permute-start | bytes 122888 | tf_op jit(solution)/shard_map/ppermute | solution.py:329
  29.4 4.4 %collective-permute-start.6 = (f32[16,640]{1,0:T(8,128)S(1)}, f32[16,640]{1,0:T(8,128)S(1)}, u32[]{:S(2)}, u32[]{:S(2)}) collective-permute-start(f32[16,640]{1,0:T(8,128)S(1)} %get-tuple-element.56), channel_id=1, source_target_pairs={{0,16},{4,20},{8,24},{12,28},{16,0},{20,4},{24,8},{28,12},{1,17},{... | collective-permute-start | bytes 122888 | tf_op jit(solution)/shard_map/ppermute | solution.py:329
  30.9 4.9 %collective-permute-start.7 = (f32[16,640]{1,0:T(8,128)S(1)}, f32[16,640]{1,0:T(8,128)S(1)}, u32[]{:S(2)}, u32[]{:S(2)}) collective-permute-start(f32[16,640]{1,0:T(8,128)S(1)} %get-tuple-element.55), channel_id=1, source_target_pairs={{0,24},{4,28},{8,16},{12,20},{16,8},{20,12},{24,0},{28,4},{1,25},{... | collective-permute-start | bytes 122888 | tf_op jit(solution)/shard_map/ppermute | solution.py:329
  35.8 8.1 %collective-permute-start.10 = (f32[16,640]{1,0:T(8,128)S(1)}, f32[16,640]{1,0:T(8,128)S(1)}, u32[]{:S(2)}, u32[]{:S(2)}) collective-permute-start(f32[16,640]{1,0:T(8,128)S(1)} %add_add_fusion.1), channel_id=1, source_target_pairs={{0,3},{1,2},{2,1},{3,0},{4,7},{5,6},{6,5},{7,4},{8,11},{9,10},{10,... | collective-permute-start | bytes 122888 | tf_op jit(solution)/shard_map/ppermute | solution.py:329
  39.5 4.5 %collective-permute-start.8 = (f32[16,640]{1,0:T(8,128)S(1)}, f32[16,640]{1,0:T(8,128)S(1)}, u32[]{:S(2)}, u32[]{:S(2)}) collective-permute-start(f32[16,640]{1,0:T(8,128)S(1)} %add_add_fusion.1), channel_id=1, source_target_pairs={{0,1},{1,0},{2,3},{3,2},{4,5},{5,4},{6,7},{7,6},{8,9},{9,8},{10,11... | collective-permute-start | bytes 122888 | tf_op jit(solution)/shard_map/ppermute | solution.py:329
  39.5 5.0 %collective-permute-start.9 = (f32[16,640]{1,0:T(8,128)S(1)}, f32[16,640]{1,0:T(8,128)S(1)}, u32[]{:S(2)}, u32[]{:S(2)}) collective-permute-start(f32[16,640]{1,0:T(8,128)S(1)} %add_add_fusion.1), channel_id=1, source_target_pairs={{0,2},{1,3},{2,0},{3,1},{4,6},{5,7},{6,4},{7,5},{8,10},{9,11},{10,... | collective-permute-start | bytes 122888 | tf_op jit(solution)/shard_map/ppermute | solution.py:329
  40.3 12.5 %collective-permute-start.3 = (f32[36,2,128]{2,1,0:T(2,128)S(1)}, f32[36,2,128]{2,1,0:T(2,128)S(1)}, u32[]{:S(2)}, u32[]{:S(2)}) collective-permute-start(f32[36,2,128]{2,1,0:T(2,128)S(1)} %pad_maximum_fusion.3), channel_id=1, source_target_pairs={{1,0},{2,1},{3,2},{0,3},{5,4},{6,5},{7,6},{4,7},{9,8},{10,9},{11,1... | collective-permute-start | bytes 110600 | tf_op jit(solution)/shard_map/ppermute | solution.py:387
  44.6 5.6 %collective-permute-start.11 = (f32[8,640]{1,0:T(8,128)S(1)}, f32[8,640]{1,0:T(8,128)S(1)}, u32[]{:S(2)}, u32[]{:S(2)}) collective-permute-start(f32[8,640]{1,0:T(8,128)S(1)} %get-tuple-element.37.zb_ref), channel_id=1, source_target_pairs={{0,8},{4,12},{8,0},{12,4},{16,24},{20,28},{24,16},{28,20},{1,9},{5... | collective-permute-start | bytes 61448 | tf_op jit(solution)/shard_map/ppermute | solution.py:329
  46.1 6.7 %collective-permute-start.2 = (f32[36,2,128]{2,1,0:T(2,128)S(1)}, f32[36,2,128]{2,1,0:T(2,128)S(1)}, u32[]{:S(2)}, u32[]{:S(2)}) collective-permute-start(f32[36,2,128]{2,1,0:T(2,128)S(1)} %pad_maximum_fusion.2), channel_id=1, source_target_pairs={{0,1},{1,2},{2,3},{3,0},{4,5},{5,6},{6,7},{7,4},{8,9},{9,10},{10,1... | collective-permute-start | bytes 110600 | tf_op jit(solution)/shard_map/ppermute | solution.py:384
  48.1 3.8 %collective-permute-start.12 = (f32[8,640]{1,0:T(8,128)S(1)}, f32[8,640]{1,0:T(8,128)S(1)}, u32[]{:S(2)}, u32[]{:S(2)}) collective-permute-start(f32[8,640]{1,0:T(8,128)S(1)} %get-tuple-element.37.zb_ref), channel_id=1, source_target_pairs={{0,16},{4,20},{8,24},{12,28},{16,0},{20,4},{24,8},{28,12},{1,17},{... | collective-permute-start | bytes 61448 | tf_op jit(solution)/shard_map/ppermute | solution.py:329
  48.1 4.7 %collective-permute-start.13 = (f32[8,640]{1,0:T(8,128)S(1)}, f32[8,640]{1,0:T(8,128)S(1)}, u32[]{:S(2)}, u32[]{:S(2)}) collective-permute-start(f32[8,640]{1,0:T(8,128)S(1)} %get-tuple-element.37.zb_ref), channel_id=1, source_target_pairs={{0,24},{4,28},{8,16},{12,20},{16,8},{20,12},{24,0},{28,4},{1,25},{... | collective-permute-start | bytes 61448 | tf_op jit(solution)/shard_map/ppermute | solution.py:329
  52.8 8.9 %collective-permute-start.14 = (f32[8,2560]{1,0:T(8,128)S(1)}, f32[8,2560]{1,0:T(8,128)}, u32[]{:S(2)}, u32[]{:S(2)}) collective-permute-start(f32[8,2560]{1,0:T(8,128)S(1)} %constant_dynamic-update-slice_fusion.4), channel_id=1, source_target_pairs={{0,4},{4,0},{8,12},{12,8},{16,20},{20,16},{24,28},{28,24},{1,5},{5... | collective-permute-start | bytes 245768 | tf_op jit(solution)/shard_map/ppermute | solution.py:329
  80.9 4.5 %collective-permute-start.15 = (f32[2,64,128]{2,1,0:T(8,128)S(1)}, f32[2,64,128]{2,1,0:T(8,128)S(1)}, u32[]{:S(2)}, u32[]{:S(2)}) collective-permute-start(f32[2,64,128]{2,1,0:T(8,128)S(1)} %get-tuple-element.45), channel_id=1, source_target_pairs={{0,4},{4,8},{8,12},{12,16},{16,20},{20,24},{24,28},{1,5},{5,9},{9,... | collective-permute-start | bytes 196616 | tf_op jit(solution)/shard_map/ppermute | solution.py:381
  83.4 2.1 %collective-permute-start.19 = (f32[8,2560]{1,0:T(8,128)S(1)}, f32[8,2560]{1,0:T(8,128)S(1)}, u32[]{:S(2)}, u32[]{:S(2)}) collective-permute-start(f32[8,2560]{1,0:T(8,128)S(1)} %constant_dynamic-slice_fusion.7), channel_id=1, source_target_pairs={{0,4},{4,0},{8,12},{12,8},{16,20},{20,16},{24,28},{28,24},{1,5},{5... | collective-permute-start | bytes 245768 | tf_op jit(solution)/shard_map/ppermute | solution.py:329
  84.2 6.9 %collective-permute-start.16 = (f32[2,64,128]{2,1,0:T(8,128)S(1)}, f32[2,64,128]{2,1,0:T(8,128)S(1)}, u32[]{:S(2)}, u32[]{:S(2)}) collective-permute-start(f32[2,64,128]{2,1,0:T(8,128)S(1)} %get-tuple-element.44), channel_id=1, source_target_pairs={{4,0},{8,4},{12,8},{16,12},{20,16},{24,20},{28,24},{5,1},{9,5},{13... | collective-permute-start | bytes 196616 | tf_op jit(solution)/shard_map/ppermute | solution.py:382
  85.5 5.6 %collective-permute-start.20 = (f32[8,640]{1,0:T(8,128)S(1)}, f32[8,640]{1,0:T(8,128)S(1)}, u32[]{:S(2)}, u32[]{:S(2)}) collective-permute-start(f32[8,640]{1,0:T(8,128)S(1)} %get-tuple-element.60), channel_id=1, source_target_pairs={{0,8},{4,12},{8,0},{12,4},{16,24},{20,28},{24,16},{28,20},{1,9},{5... | collective-permute-start | bytes 61448 | tf_op jit(solution)/shard_map/ppermute | solution.py:329
  88.6 3.8 %collective-permute-start.21 = (f32[8,640]{1,0:T(8,128)S(1)}, f32[8,640]{1,0:T(8,128)S(1)}, u32[]{:S(2)}, u32[]{:S(2)}) collective-permute-start(f32[8,640]{1,0:T(8,128)S(1)} %get-tuple-element.62), channel_id=1, source_target_pairs={{0,16},{4,20},{8,24},{12,28},{16,0},{20,4},{24,8},{28,12},{1,17},{... | collective-permute-start | bytes 61448 | tf_op jit(solution)/shard_map/ppermute | solution.py:329
  89.7 4.7 %collective-permute-start.22 = (f32[8,640]{1,0:T(8,128)S(1)}, f32[8,640]{1,0:T(8,128)S(1)}, u32[]{:S(2)}, u32[]{:S(2)}) collective-permute-start(f32[8,640]{1,0:T(8,128)S(1)} %get-tuple-element.61), channel_id=1, source_target_pairs={{0,24},{4,28},{8,16},{12,20},{16,8},{20,12},{24,0},{28,4},{1,25},{... | collective-permute-start | bytes 61448 | tf_op jit(solution)/shard_map/ppermute | solution.py:329
  94.4 6.4 %collective-permute-start.23 = (f32[8,640]{1,0:T(8,128)S(1)}, f32[8,640]{1,0:T(8,128)S(1)}, u32[]{:S(2)}, u32[]{:S(2)}) collective-permute-start(f32[8,640]{1,0:T(8,128)S(1)} %add_add_fusion.4), channel_id=1, source_target_pairs={{0,1},{1,0},{2,3},{3,2},{4,5},{5,4},{6,7},{7,6},{8,9},{9,8},{10,11... | collective-permute-start | bytes 61448 | tf_op jit(solution)/shard_map/ppermute | solution.py:329
  94.5 6.3 %collective-permute-start.24 = (f32[8,640]{1,0:T(8,128)S(1)}, f32[8,640]{1,0:T(8,128)S(1)}, u32[]{:S(2)}, u32[]{:S(2)}) collective-permute-start(f32[8,640]{1,0:T(8,128)S(1)} %add_add_fusion.4), channel_id=1, source_target_pairs={{0,2},{1,3},{2,0},{3,1},{4,6},{5,7},{6,4},{7,5},{8,10},{9,11},{10,... | collective-permute-start | bytes 61448 | tf_op jit(solution)/shard_map/ppermute | solution.py:329
  96.9 5.6 %collective-permute-start.25 = (f32[8,640]{1,0:T(8,128)S(1)}, f32[8,640]{1,0:T(8,128)S(1)}, u32[]{:S(2)}, u32[]{:S(2)}) collective-permute-start(f32[8,640]{1,0:T(8,128)S(1)} %add_add_fusion.4), channel_id=1, source_target_pairs={{0,3},{1,2},{2,1},{3,0},{4,7},{5,6},{6,5},{7,4},{8,11},{9,10},{10,... | collective-permute-start | bytes 61448 | tf_op jit(solution)/shard_map/ppermute | solution.py:329
  98.9 12.4 %collective-permute-start.18 = (f32[36,2,128]{2,1,0:T(2,128)S(1)}, f32[36,2,128]{2,1,0:T(2,128)S(1)}, u32[]{:S(2)}, u32[]{:S(2)}) collective-permute-start(f32[36,2,128]{2,1,0:T(2,128)S(1)} %pad_maximum_fusion.5), channel_id=1, source_target_pairs={{1,0},{2,1},{3,2},{0,3},{5,4},{6,5},{7,6},{4,7},{9,8},{10,9},{11,1... | collective-permute-start | bytes 110600 | tf_op jit(solution)/shard_map/ppermute | solution.py:387
  103.8 3.8 %collective-permute-start.26 = (f32[8,640]{1,0:T(8,128)S(1)}, f32[8,640]{1,0:T(8,128)S(1)}, u32[]{:S(2)}, u32[]{:S(2)}) collective-permute-start(f32[8,640]{1,0:T(8,128)S(1)} %get-tuple-element.34.ub_ref), channel_id=1, source_target_pairs={{0,8},{4,12},{8,0},{12,4},{16,24},{20,28},{24,16},{28,20},{1,9},{5... | collective-permute-start | bytes 61448 | tf_op jit(solution)/shard_map/ppermute | solution.py:329
  105.8 6.1 %collective-permute-start.17 = (f32[36,2,128]{2,1,0:T(2,128)S(1)}, f32[36,2,128]{2,1,0:T(2,128)S(1)}, u32[]{:S(2)}, u32[]{:S(2)}) collective-permute-start(f32[36,2,128]{2,1,0:T(2,128)S(1)} %pad_maximum_fusion.4), channel_id=1, source_target_pairs={{0,1},{1,2},{2,3},{3,0},{4,5},{5,6},{6,7},{7,4},{8,9},{9,10},{10,1... | collective-permute-start | bytes 110600 | tf_op jit(solution)/shard_map/ppermute | solution.py:384
  105.8 3.8 %collective-permute-start.27 = (f32[8,640]{1,0:T(8,128)S(1)}, f32[8,640]{1,0:T(8,128)S(1)}, u32[]{:S(2)}, u32[]{:S(2)}) collective-permute-start(f32[8,640]{1,0:T(8,128)S(1)} %get-tuple-element.34.ub_ref), channel_id=1, source_target_pairs={{0,16},{4,20},{8,24},{12,28},{16,0},{20,4},{24,8},{28,12},{1,17},{... | collective-permute-start | bytes 61448 | tf_op jit(solution)/shard_map/ppermute | solution.py:329
  105.9 4.7 %collective-permute-start.28 = (f32[8,640]{1,0:T(8,128)S(1)}, f32[8,640]{1,0:T(8,128)S(1)}, u32[]{:S(2)}, u32[]{:S(2)}) collective-permute-start(f32[8,640]{1,0:T(8,128)S(1)} %get-tuple-element.34.ub_ref), channel_id=1, source_target_pairs={{0,24},{4,28},{8,16},{12,20},{16,8},{20,12},{24,0},{28,4},{1,25},{... | collective-permute-start | bytes 61448 | tf_op jit(solution)/shard_map/ppermute | solution.py:329
  111.3 12.3 %collective-permute-start.29 = (f32[8,2560]{1,0:T(8,128)}, f32[8,2560]{1,0:T(8,128)}, u32[]{:S(2)}, u32[]{:S(2)}) collective-permute-start(f32[8,2560]{1,0:T(8,128)} %constant_dynamic-update-slice_fusion), channel_id=1, source_target_pairs={{0,4},{4,0},{8,12},{12,8},{16,20},{20,16},{24,28},{28,24},{1,5},{5... | collective-permute-start | bytes 245768 | tf_op jit(solution)/shard_map/ppermute | solution.py:329
  145.6 4.3 %collective-permute-start.30 = (f32[1,64,128]{2,1,0:T(8,128)S(1)}, f32[1,64,128]{2,1,0:T(8,128)S(1)}, u32[]{:S(2)}, u32[]{:S(2)}) collective-permute-start(f32[1,64,128]{2,1,0:T(8,128)S(1)} %get-tuple-element.41), channel_id=1, source_target_pairs={{0,4},{4,8},{8,12},{12,16},{16,20},{20,24},{24,28},{1,5},{5,9},{9,... | collective-permute-start | bytes 98312 | tf_op jit(solution)/shard_map/ppermute | solution.py:381
  148.1 3.6 %collective-permute-start.34 = (f32[8,2560]{1,0:T(8,128)S(1)}, f32[8,2560]{1,0:T(8,128)S(1)}, u32[]{:S(2)}, u32[]{:S(2)}) collective-permute-start(f32[8,2560]{1,0:T(8,128)S(1)} %constant_dynamic-slice_fusion.3), channel_id=1, source_target_pairs={{0,4},{4,0},{8,12},{12,8},{16,20},{20,16},{24,28},{28,24},{1,5},{5... | collective-permute-start | bytes 245768 | tf_op jit(solution)/shard_map/ppermute | solution.py:329
  148.6 3.1 %collective-permute-start.31 = (f32[1,64,128]{2,1,0:T(8,128)S(1)}, f32[1,64,128]{2,1,0:T(8,128)S(1)}, u32[]{:S(2)}, u32[]{:S(2)}) collective-permute-start(f32[1,64,128]{2,1,0:T(8,128)S(1)} %get-tuple-element.40), channel_id=1, source_target_pairs={{4,0},{8,4},{12,8},{16,12},{20,16},{24,20},{28,24},{5,1},{9,5},{13... | collective-permute-start | bytes 98312 | tf_op jit(solution)/shard_map/ppermute | solution.py:382
  151.7 9.4 %collective-permute-start.35 = (f32[8,640]{1,0:T(8,128)S(1)}, f32[8,640]{1,0:T(8,128)S(1)}, u32[]{:S(2)}, u32[]{:S(2)}) collective-permute-start(f32[8,640]{1,0:T(8,128)S(1)} %get-tuple-element.57), channel_id=1, source_target_pairs={{0,8},{4,12},{8,0},{12,4},{16,24},{20,28},{24,16},{28,20},{1,9},{5... | collective-permute-start | bytes 61448 | tf_op jit(solution)/shard_map/ppermute | solution.py:329
  154.7 6.4 %collective-permute-start.36 = (f32[8,640]{1,0:T(8,128)S(1)}, f32[8,640]{1,0:T(8,128)S(1)}, u32[]{:S(2)}, u32[]{:S(2)}) collective-permute-start(f32[8,640]{1,0:T(8,128)S(1)} %get-tuple-element.59), channel_id=1, source_target_pairs={{0,16},{4,20},{8,24},{12,28},{16,0},{20,4},{24,8},{28,12},{1,17},{... | collective-permute-start | bytes 61448 | tf_op jit(solution)/shard_map/ppermute | solution.py:329
  155.9 5.2 %collective-permute-start.37 = (f32[8,640]{1,0:T(8,128)S(1)}, f32[8,640]{1,0:T(8,128)S(1)}, u32[]{:S(2)}, u32[]{:S(2)}) collective-permute-start(f32[8,640]{1,0:T(8,128)S(1)} %get-tuple-element.58), channel_id=1, source_target_pairs={{0,24},{4,28},{8,16},{12,20},{16,8},{20,12},{24,0},{28,4},{1,25},{... | collective-permute-start | bytes 61448 | tf_op jit(solution)/shard_map/ppermute | solution.py:329
  157.3 13.3 %collective-permute-start.33 = (f32[34,1,128]{2,1,0:T(1,128)S(1)}, f32[34,1,128]{2,1,0:T(1,128)S(1)}, u32[]{:S(2)}, u32[]{:S(2)}) collective-permute-start(f32[34,1,128]{2,1,0:T(1,128)S(1)} %pad_maximum_fusion.7), channel_id=1, source_target_pairs={{1,0},{2,1},{3,2},{0,3},{5,4},{6,5},{7,6},{4,7},{9,8},{10,9},{11,1... | collective-permute-start | bytes 52232 | tf_op jit(solution)/shard_map/ppermute | solution.py:387
  161.1 4.5 %collective-permute-start.38 = (f32[8,640]{1,0:T(8,128)S(1)}, f32[8,640]{1,0:T(8,128)S(1)}, u32[]{:S(2)}, u32[]{:S(2)}) collective-permute-start(f32[8,640]{1,0:T(8,128)S(1)} %add_add_fusion.3), channel_id=1, source_target_pairs={{0,1},{1,0},{2,3},{3,2},{4,5},{5,4},{6,7},{7,6},{8,9},{9,8},{10,11... | collective-permute-start | bytes 61448 | tf_op jit(solution)/shard_map/ppermute | solution.py:329
  161.2 5.5 %collective-permute-start.39 = (f32[8,640]{1,0:T(8,128)S(1)}, f32[8,640]{1,0:T(8,128)S(1)}, u32[]{:S(2)}, u32[]{:S(2)}) collective-permute-start(f32[8,640]{1,0:T(8,128)S(1)} %add_add_fusion.3), channel_id=1, source_target_pairs={{0,2},{1,3},{2,0},{3,1},{4,6},{5,7},{6,4},{7,5},{8,10},{9,11},{10,... | collective-permute-start | bytes 61448 | tf_op jit(solution)/shard_map/ppermute | solution.py:329
  165.0 5.6 %collective-permute-start.40 = (f32[8,640]{1,0:T(8,128)S(1)}, f32[8,640]{1,0:T(8,128)S(1)}, u32[]{:S(2)}, u32[]{:S(2)}) collective-permute-start(f32[8,640]{1,0:T(8,128)S(1)} %add_add_fusion.3), channel_id=1, source_target_pairs={{0,3},{1,2},{2,1},{3,0},{4,7},{5,6},{6,5},{7,4},{8,11},{9,10},{10,... | collective-permute-start | bytes 61448 | tf_op jit(solution)/shard_map/ppermute | solution.py:329
  165.6 5.6 %collective-permute-start.32 = (f32[34,1,128]{2,1,0:T(1,128)S(1)}, f32[34,1,128]{2,1,0:T(1,128)S(1)}, u32[]{:S(2)}, u32[]{:S(2)}) collective-permute-start(f32[34,1,128]{2,1,0:T(1,128)S(1)} %pad_maximum_fusion.6), channel_id=1, source_target_pairs={{0,1},{1,2},{2,3},{3,0},{4,5},{5,6},{6,7},{7,4},{8,9},{9,10},{10,1... | collective-permute-start | bytes 52232 | tf_op jit(solution)/shard_map/ppermute | solution.py:384
  172.5 1.2 collective-permute-start.41
  173.8 3.7 %collective-permute-start.42 = (f32[16,128]{1,0:T(8,128)S(1)}, f32[16,128]{1,0:T(8,128)S(1)}, u32[]{:S(2)}, u32[]{:S(2)}) collective-permute-start(f32[16,128]{1,0:T(8,128)S(1)} %add.157), channel_id=1, source_target_pairs={{0,8},{4,12},{8,0},{12,4},{16,24},{20,28},{24,16},{28,20},{1,9},{5... | collective-permute-start | bytes 24584 | tf_op jit(solution)/shard_map/ppermute | solution.py:329
  175.2 3.7 %collective-permute-start.43 = (f32[16,128]{1,0:T(8,128)S(1)}, f32[16,128]{1,0:T(8,128)S(1)}, u32[]{:S(2)}, u32[]{:S(2)}) collective-permute-start(f32[16,128]{1,0:T(8,128)S(1)} %add.157), channel_id=1, source_target_pairs={{0,16},{4,20},{8,24},{12,28},{16,0},{20,4},{24,8},{28,12},{1,17},{... | collective-permute-start | bytes 24584 | tf_op jit(solution)/shard_map/ppermute | solution.py:329
  175.9 4.5 %collective-permute-start.44 = (f32[16,128]{1,0:T(8,128)S(1)}, f32[16,128]{1,0:T(8,128)S(1)}, u32[]{:S(2)}, u32[]{:S(2)}) collective-permute-start(f32[16,128]{1,0:T(8,128)S(1)} %add.157), channel_id=1, source_target_pairs={{0,24},{4,28},{8,16},{12,20},{16,8},{20,12},{24,0},{28,4},{1,25},{... | collective-permute-start | bytes 24584 | tf_op jit(solution)/shard_map/ppermute | solution.py:329
  180.4 4.4 %collective-permute-start.45 = (f32[16,128]{1,0:T(8,128)S(1)}, f32[16,128]{1,0:T(8,128)S(1)}, u32[]{:S(2)}, u32[]{:S(2)}) collective-permute-start(f32[16,128]{1,0:T(8,128)S(1)} %add_add_fusion.5.refs_0_), channel_id=1, source_target_pairs={{0,1},{1,0},{2,3},{3,2},{4,5},{5,4},{6,7},{7,6},{8,9},{9,8},{10,11... | collective-permute-start | bytes 24584 | tf_op jit(solution)/shard_map/ppermute | solution.py:329
  180.4 4.6 %collective-permute-start.46 = (f32[16,128]{1,0:T(8,128)S(1)}, f32[16,128]{1,0:T(8,128)S(1)}, u32[]{:S(2)}, u32[]{:S(2)}) collective-permute-start(f32[16,128]{1,0:T(8,128)S(1)} %add_add_fusion.5.refs_0_), channel_id=1, source_target_pairs={{0,2},{1,3},{2,0},{3,1},{4,6},{5,7},{6,4},{7,5},{8,10},{9,11},{10,... | collective-permute-start | bytes 24584 | tf_op jit(solution)/shard_map/ppermute | solution.py:329
  182.2 5.4 %collective-permute-start.47 = (f32[16,128]{1,0:T(8,128)S(1)}, f32[16,128]{1,0:T(8,128)S(1)}, u32[]{:S(2)}, u32[]{:S(2)}) collective-permute-start(f32[16,128]{1,0:T(8,128)S(1)} %add_add_fusion.5.refs_0_), channel_id=1, source_target_pairs={{0,3},{1,2},{2,1},{3,0},{4,7},{5,6},{6,5},{7,4},{8,11},{9,10},{10,... | collective-permute-start | bytes 24584 | tf_op jit(solution)/shard_map/ppermute | solution.py:329
  (25 other events, 369.1 us)
